TPU v7x, 16 devices: a 4x2x1 block of a 4x4x8 slice. The times are simulated.
16 devices in a mesh: dp: 2 (over y, z), cp: 8 (over x, core).
Axes of the slice: x: 4, y: 2, z: 1, core: 2. Of those that a mesh axis runs over, the one named last changes fastest.
The devices are a block of a 4x4x8 slice.
Arguments:
- x_in: bfloat16 [1024, 2048], P(('dp', 'cp')), parts along dimension 0
- cache_k1: bfloat16 [32768, 2, 128], P(('dp', 'cp')), parts along dimension 0
- cache_v1: bfloat16 [32768, 2, 128], P(('dp', 'cp')), parts along dimension 0
- w_q1: bfloat16 [2048, 2048], replicated
- b_q1: bfloat16 [2048], replicated
- w_k1: bfloat16 [2048, 256], replicated
- b_k1: bfloat16 [256], replicated
- w_v1: bfloat16 [2048, 256], replicated
- w_o1: bfloat16 [2048, 2048], replicated
- w_gate: bfloat16 [2048, 11008], replicated
- w_up: bfloat16 [2048, 11008], replicated
- w_down: bfloat16 [11008, 2048], replicated
- cache_k2: bfloat16 [32768, 2, 128], P(('dp', 'cp')), parts along dimension 0
- cache_v2: bfloat16 [32768, 2, 128], P(('dp', 'cp')), parts along dimension 0
- w_q2: bfloat16 [2048, 2048], replicated
- b_q2: bfloat16 [2048], replicated
- w_k2: bfloat16 [2048, 256], replicated
- b_k2: bfloat16 [256], replicated
- w_v2: bfloat16 [2048, 256], replicated
- w_o2: bfloat16 [2048, 2048], replicated
Outputs:
- output 1: bfloat16 [1024, 2048], P(('dp', 'cp')), parts along dimension 0
- output 2: bfloat16 [1024, 2048], P(('dp', 'cp')), parts along dimension 0
- output 3: bfloat16 [1024, 2, 128], P(('dp', 'cp')), parts along dimension 0
- output 4: bfloat16 [1024, 2, 128], P(('dp', 'cp')), parts along dimension 0
- output 5: bfloat16 [1024, 2, 128], P(('dp', 'cp')), parts along dimension 0
- output 6: bfloat16 [1024, 2, 128], P(('dp', 'cp')), parts along dimension 0
There are 2 independent parts. A program takes and returns all parts, laid end to end along the dimension named above; an argument that names none is the same for every part.
All inputs are finite; a program needn't handle non-finite values.
Results may differ from a plain program's by a relative error of at most 0.0144509.
Values are sent between devices in bfloat16 or wider.
A program may use at most 768 MiB of HBM per device.

v0:
```python
import jax
import jax.numpy as jnp
from jax import lax
from jax.sharding import PartitionSpec as P

ROPE_THETA = 500000.0
NORM_EPS = 1e-5


def rms_norm(vals):
    wide = vals.astype(jnp.float32)
    return (wide * lax.rsqrt(jnp.mean(wide * wide, axis=-1, keepdims=True) + NORM_EPS)).astype(jnp.bfloat16)


def rope_tables(positions, head_dim):
    half_dim = head_dim // 2
    inv_freq = 1.0 / (ROPE_THETA ** (jnp.arange(half_dim, dtype=jnp.float32) * (2.0 / head_dim)))
    angles = positions.astype(jnp.float32)[:, None] * inv_freq[None, :]
    return jnp.cos(angles)[:, None, :], jnp.sin(angles)[:, None, :]


def apply_rope(vals, cos_t, sin_t):
    half_dim = vals.shape[-1] // 2
    first = vals[..., :half_dim]
    second = vals[..., half_dim:]
    return jnp.concatenate([first * cos_t - second * sin_t, second * cos_t + first * sin_t], axis=-1)


def project_rows(layer_in, w_q, b_q, w_k, b_k, w_v, positions, head_dim):
    rows = layer_in.shape[0]
    cos_t, sin_t = rope_tables(positions, head_dim)
    q_pre = (jnp.dot(layer_in, w_q, preferred_element_type=jnp.float32) + b_q.astype(jnp.float32)).astype(jnp.bfloat16)
    k_pre = (jnp.dot(layer_in, w_k, preferred_element_type=jnp.float32) + b_k.astype(jnp.float32)).astype(jnp.bfloat16)
    v_new = jnp.dot(layer_in, w_v, preferred_element_type=jnp.float32).astype(jnp.bfloat16).reshape(rows, -1, head_dim)
    q_rot = apply_rope(q_pre.reshape(rows, -1, head_dim).astype(jnp.float32), cos_t, sin_t).astype(jnp.bfloat16)
    k_new = apply_rope(k_pre.reshape(rows, -1, head_dim).astype(jnp.float32), cos_t, sin_t).astype(jnp.bfloat16)
    return q_rot, k_new, v_new


def mlp_block(resid_h, w_gate, w_up, w_down):
    normed = rms_norm(resid_h)
    gate_act = jnp.dot(normed, w_gate, preferred_element_type=jnp.float32).astype(jnp.bfloat16)
    up_proj = jnp.dot(normed, w_up, preferred_element_type=jnp.float32).astype(jnp.bfloat16)
    mixed = (jax.nn.silu(gate_act.astype(jnp.float32)) * up_proj.astype(jnp.float32)).astype(jnp.bfloat16)
    return (resid_h.astype(jnp.float32) + jnp.dot(mixed, w_down, preferred_element_type=jnp.float32)).astype(jnp.bfloat16)


def partial_attend(q_grp, keys, values, scale, visible):
    scores = jnp.einsum('tkgd,skd->tkgs', q_grp, keys, preferred_element_type=jnp.float32) * scale
    if visible is not None:
        scores = jnp.where(visible, scores, -jnp.inf)
    peak = jnp.max(scores, axis=-1)
    prob_w = jnp.exp(scores - peak[..., None])
    total = jnp.sum(prob_w, axis=-1)
    summed = jnp.einsum('tkgs,skd->tkgd', prob_w.astype(jnp.bfloat16), values, preferred_element_type=jnp.float32)
    return summed / total[..., None], peak + jnp.log(total)


def merge_parts(out_a, lse_a, out_b, lse_b):
    lse_new = jnp.logaddexp(lse_a, lse_b)
    merged = out_a * jnp.exp(lse_a - lse_new)[..., None] + out_b * jnp.exp(lse_b - lse_new)[..., None]
    return merged, lse_new


def attention_layer(layer_in, cache_k, cache_v, w_q, b_q, w_k, b_k, w_v, w_o, axis_size):
    tok_dev = layer_in.shape[0]
    cache_dev, kv_heads, head_dim = cache_k.shape
    heads = w_q.shape[1] // head_dim
    my_idx = lax.axis_index('cp')
    positions = axis_size * cache_dev + my_idx * tok_dev + jnp.arange(tok_dev)
    q_rot, k_new, v_new = project_rows(layer_in, w_q, b_q, w_k, b_k, w_v, positions, head_dim)
    q_grp = q_rot.reshape(tok_dev, kv_heads, heads // kv_heads, head_dim)
    scale = head_dim ** -0.5
    all_k = lax.all_gather(k_new, 'cp', axis=0, tiled=True)
    all_v = lax.all_gather(v_new, 'cp', axis=0, tiled=True)
    q_pos = my_idx * tok_dev + jnp.arange(tok_dev)
    visible = (jnp.arange(axis_size * tok_dev)[None, :] <= q_pos[:, None])[:, None, None, :]
    out_acc, lse_acc = partial_attend(q_grp, all_k, all_v, scale, visible)
    out_loc, lse_loc = partial_attend(q_grp, cache_k, cache_v, scale, None)
    out_acc, lse_acc = merge_parts(out_acc, lse_acc, out_loc, lse_loc)
    shift = [(src_idx, (src_idx + 1) % axis_size) for src_idx in range(axis_size)]

    def cache_step(step, carry):
        blk_k, blk_v, out_run, lse_run = carry
        blk_k = lax.ppermute(blk_k, 'cp', shift)
        blk_v = lax.ppermute(blk_v, 'cp', shift)
        out_blk, lse_blk = partial_attend(q_grp, blk_k, blk_v, scale, None)
        out_run, lse_run = merge_parts(out_run, lse_run, out_blk, lse_blk)
        return blk_k, blk_v, out_run, lse_run

    carry_end = lax.fori_loop(0, axis_size - 1, cache_step, (cache_k, cache_v, out_acc, lse_acc))
    o_half = carry_end[2].astype(jnp.bfloat16).reshape(tok_dev, heads * head_dim)
    y_out = jnp.dot(o_half, w_o, preferred_element_type=jnp.float32).astype(jnp.bfloat16)
    return y_out, k_new, v_new


def solution(mesh):
    axis_size = mesh.shape['cp']
    rows_spec = P(('dp', 'cp'), None)
    cache_spec = P(('dp', 'cp'), None, None)
    mat_spec = P(None, None)
    vec_spec = P(None)
    layer_specs = (cache_spec, cache_spec, mat_spec, vec_spec, mat_spec, vec_spec, mat_spec, mat_spec)
    in_specs = (rows_spec,) + layer_specs + (mat_spec, mat_spec, mat_spec) + layer_specs
    out_specs = (rows_spec, rows_spec, cache_spec, cache_spec, cache_spec, cache_spec)

    def forward(x_in, cache_k1, cache_v1, w_q1, b_q1, w_k1, b_k1, w_v1, w_o1, w_gate, w_up, w_down, cache_k2, cache_v2, w_q2, b_q2, w_k2, b_k2, w_v2, w_o2):
        y_one, k_one, v_one = attention_layer(x_in, cache_k1, cache_v1, w_q1, b_q1, w_k1, b_k1, w_v1, w_o1, axis_size)
        resid_h = (x_in.astype(jnp.float32) + y_one.astype(jnp.float32)).astype(jnp.bfloat16)
        hidden = mlp_block(resid_h, w_gate, w_up, w_down)
        y_two, k_two, v_two = attention_layer(rms_norm(hidden), cache_k2, cache_v2, w_q2, b_q2, w_k2, b_k2, w_v2, w_o2, axis_size)
        return hidden, y_two, k_one, v_one, k_two, v_two

    return jax.shard_map(forward, mesh=mesh, in_specs=in_specs, out_specs=out_specs, check_vma=False)
```

profile of v0, /device:TPU:113, one launch (start us, length us, event | category | flops | bytes accessed | tf_op | source)
XLA Modules:
  0.0 623.3 jit_solution(18265754665487326299)
XLA Ops:
  3.4 19.2 %all_gather.13 = bf16[512,2,128]{2,0,1:T(8,128)(2,1)S(1)} all-gather(bf16[64,2,128]{2,0,1:T(8,128)(2,1)S(1)} %pad_maximum_fusion.2), channel_id=1, replica_groups=mesh['dp'=2,'cp'=8] {'cp'}, dimensions={0}, use_global_device_ids=true | all-gather | bytes 294912 | tf_op jit(solution)/shard_map/all_gather | solution.py:74
  23.3 5.0 fusion.98
  32.4 3.2 copy-done.3
  37.5 5.0 fusion.71
  43.4 21.8 %all_gather.12 = bf16[512,2,128]{2,0,1:T(8,128)(2,1)S(1)} all-gather(bf16[64,2,128]{2,0,1:T(8,128)(2,1)S(1)} %copy_bitcast_fusion.1), channel_id=1, replica_groups=mesh['dp'=2,'cp'=8] {'cp'}, dimensions={0}, use_global_device_ids=true | all-gather | bytes 294912 | tf_op jit(solution)/shard_map/all_gather | solution.py:75
  70.8 207.0 %while.32 = (s32[]{:T(128)}, bf16[2048,2,128]{2,0,1:T(8,128)(2,1)}, bf16[2048,2,128]{2,0,1:T(8,128)(2,1)}, f32[64,2,8,128]{3,0,2,1:T(8,128)S(1)}, f32[64,2,8]{0,...) while((s32[]{:T(128)}, bf16[2048,2,128]{2,0,1:T(8,128)(2,1)}, ...), condition=%wide.region_7.8_spmd, body=%wide.region_4.7_spmd.sunk | while | flops 1091053568 | bytes 41222300 | solution.py:91
  70.8 6.8 %collective-permute-start = (bf16[2048,2,128]{2,0,1:T(8,128)(2,1)}, bf16[2048,2,128]{2,0,1:T(8,128)(2,1)S(1)}, u32[]{:S(2)}, u32[]{:S(2)}) collective-permute-start(bf16[2048,2,128]{2,0,1:T(8,128)(2,1)} %get-tuple-element.304), channel_id=1, source_target_pairs={{0,1},{1,2},{2,3},{3,4},{4,5},{5,6},{6,7},{7,0},{8,9},{9,10},{10,1... | collective-permute-start | bytes 3145736 | tf_op jit(solution)/shard_map/while/body/eval_jaxpr/ppermute | solution.py:85
  77.6 11.7 %collective-permute-done = bf16[2048,2,128]{2,0,1:T(8,128)(2,1)S(1)} collective-permute-done((bf16[2048,2,128]{2,0,1:T(8,128)(2,1)}, bf16[2048,2,128]{2,0,1:T(8,128)(2,1)S(1)}, u32[]{:S(2)}, u32[]{:S(2)}) %collective-permute-start) | collective-permute-done | bytes 1048608 | tf_op jit(solution)/shard_map/while/body/eval_jaxpr/ppermute | solution.py:85
  93.4 7.2 %collective-permute-done.1 = bf16[2048,2,128]{2,0,1:T(8,128)(2,1)S(1)} collective-permute-done((bf16[2048,2,128]{2,0,1:T(8,128)(2,1)}, bf16[2048,2,128]{2,0,1:T(8,128)(2,1)S(1)}, u32[]{:S(2)}, u32[]{:S(2)}) %collective-permute-start.1) | collective-permute-done | bytes 1048608 | tf_op jit(solution)/shard_map/while/body/eval_jaxpr/ppermute | solution.py:86
  104.1 2.5 collective-permute-start
  106.7 11.7 %collective-permute-done = bf16[2048,2,128]{2,0,1:T(8,128)(2,1)S(1)} collective-permute-done((bf16[2048,2,128]{2,0,1:T(8,128)(2,1)}, bf16[2048,2,128]{2,0,1:T(8,128)(2,1)S(1)}, u32[]{:S(2)}, u32[]{:S(2)}) %collective-permute-start) | collective-permute-done | bytes 1048608 | tf_op jit(solution)/shard_map/while/body/eval_jaxpr/ppermute | solution.py:85
  122.3 7.2 %collective-permute-done.1 = bf16[2048,2,128]{2,0,1:T(8,128)(2,1)S(1)} collective-permute-done((bf16[2048,2,128]{2,0,1:T(8,128)(2,1)}, bf16[2048,2,128]{2,0,1:T(8,128)(2,1)S(1)}, u32[]{:S(2)}, u32[]{:S(2)}) %collective-permute-start.1) | collective-permute-done | bytes 1048608 | tf_op jit(solution)/shard_map/while/body/eval_jaxpr/ppermute | solution.py:86
  133.0 2.5 collective-permute-start
  135.6 11.7 %collective-permute-done = bf16[2048,2,128]{2,0,1:T(8,128)(2,1)S(1)} collective-permute-done((bf16[2048,2,128]{2,0,1:T(8,128)(2,1)}, bf16[2048,2,128]{2,0,1:T(8,128)(2,1)S(1)}, u32[]{:S(2)}, u32[]{:S(2)}) %collective-permute-start) | collective-permute-done | bytes 1048608 | tf_op jit(solution)/shard_map/while/body/eval_jaxpr/ppermute | solution.py:85
  151.3 7.2 %collective-permute-done.1 = bf16[2048,2,128]{2,0,1:T(8,128)(2,1)S(1)} collective-permute-done((bf16[2048,2,128]{2,0,1:T(8,128)(2,1)}, bf16[2048,2,128]{2,0,1:T(8,128)(2,1)S(1)}, u32[]{:S(2)}, u32[]{:S(2)}) %collective-permute-start.1) | collective-permute-done | bytes 1048608 | tf_op jit(solution)/shard_map/while/body/eval_jaxpr/ppermute | solution.py:86
  162.0 2.6 collective-permute-start
  164.6 11.7 %collective-permute-done = bf16[2048,2,128]{2,0,1:T(8,128)(2,1)S(1)} collective-permute-done((bf16[2048,2,128]{2,0,1:T(8,128)(2,1)}, bf16[2048,2,128]{2,0,1:T(8,128)(2,1)S(1)}, u32[]{:S(2)}, u32[]{:S(2)}) %collective-permute-start) | collective-permute-done | bytes 1048608 | tf_op jit(solution)/shard_map/while/body/eval_jaxpr/ppermute | solution.py:85
  180.3 7.2 %collective-permute-done.1 = bf16[2048,2,128]{2,0,1:T(8,128)(2,1)S(1)} collective-permute-done((bf16[2048,2,128]{2,0,1:T(8,128)(2,1)}, bf16[2048,2,128]{2,0,1:T(8,128)(2,1)S(1)}, u32[]{:S(2)}, u32[]{:S(2)}) %collective-permute-start.1) | collective-permute-done | bytes 1048608 | tf_op jit(solution)/shard_map/while/body/eval_jaxpr/ppermute | solution.py:86
  190.9 2.5 collective-permute-start
  193.5 11.7 %collective-permute-done = bf16[2048,2,128]{2,0,1:T(8,128)(2,1)S(1)} collective-permute-done((bf16[2048,2,128]{2,0,1:T(8,128)(2,1)}, bf16[2048,2,128]{2,0,1:T(8,128)(2,1)S(1)}, u32[]{:S(2)}, u32[]{:S(2)}) %collective-permute-start) | collective-permute-done | bytes 1048608 | tf_op jit(solution)/shard_map/while/body/eval_jaxpr/ppermute | solution.py:85
  209.2 7.2 %collective-permute-done.1 = bf16[2048,2,128]{2,0,1:T(8,128)(2,1)S(1)} collective-permute-done((bf16[2048,2,128]{2,0,1:T(8,128)(2,1)}, bf16[2048,2,128]{2,0,1:T(8,128)(2,1)S(1)}, u32[]{:S(2)}, u32[]{:S(2)}) %collective-permute-start.1) | collective-permute-done | bytes 1048608 | tf_op jit(solution)/shard_map/while/body/eval_jaxpr/ppermute | solution.py:86
  219.9 2.5 collective-permute-start
  222.5 11.7 %collective-permute-done = bf16[2048,2,128]{2,0,1:T(8,128)(2,1)S(1)} collective-permute-done((bf16[2048,2,128]{2,0,1:T(8,128)(2,1)}, bf16[2048,2,128]{2,0,1:T(8,128)(2,1)S(1)}, u32[]{:S(2)}, u32[]{:S(2)}) %collective-permute-start) | collective-permute-done | bytes 1048608 | tf_op jit(solution)/shard_map/while/body/eval_jaxpr/ppermute | solution.py:85
  238.2 7.2 %collective-permute-done.1 = bf16[2048,2,128]{2,0,1:T(8,128)(2,1)S(1)} collective-permute-done((bf16[2048,2,128]{2,0,1:T(8,128)(2,1)}, bf16[2048,2,128]{2,0,1:T(8,128)(2,1)S(1)}, u32[]{:S(2)}, u32[]{:S(2)}) %collective-permute-start.1) | collective-permute-done | bytes 1048608 | tf_op jit(solution)/shard_map/while/body/eval_jaxpr/ppermute | solution.py:86
  248.9 2.6 collective-permute-start
  251.5 11.7 %collective-permute-done = bf16[2048,2,128]{2,0,1:T(8,128)(2,1)S(1)} collective-permute-done((bf16[2048,2,128]{2,0,1:T(8,128)(2,1)}, bf16[2048,2,128]{2,0,1:T(8,128)(2,1)S(1)}, u32[]{:S(2)}, u32[]{:S(2)}) %collective-permute-start) | collective-permute-done | bytes 1048608 | tf_op jit(solution)/shard_map/while/body/eval_jaxpr/ppermute | solution.py:85
  267.2 7.2 %collective-permute-done.1 = bf16[2048,2,128]{2,0,1:T(8,128)(2,1)S(1)} collective-permute-done((bf16[2048,2,128]{2,0,1:T(8,128)(2,1)}, bf16[2048,2,128]{2,0,1:T(8,128)(2,1)S(1)}, u32[]{:S(2)}, u32[]{:S(2)}) %collective-permute-start.1) | collective-permute-done | bytes 1048608 | tf_op jit(solution)/shard_map/while/body/eval_jaxpr/ppermute | solution.py:86
  278.0 5.1 multiply_reduce_fusion
  283.1 19.5 %fusion.61 = f32[64,11008]{1,0:T(8,128)} fusion(bf16[2048,11008]{1,0:T(8,128)(2,1)} %param.33, f32[64,2048]{1,0:T(8,128)S(1)} %get-tuple-element.199, f32[64]{0:T(128)S(1)} %add_rsqrt_fusion.1), kind=kOutput, calls=%fused_computation.45 | convolution fusion | flops 2887352320 | bytes 48431360 | tf_op jit(solution)/shard_map/dot_general | solution.py:42
  302.6 32.3 %fusion.119 = (f32[64]{0:T(128)S(1)}, bf16[64,2048]{1,0:T(8,128)(2,1)S(1)}) fusion(f32[64,2048]{1,0:T(8,128)S(1)} %get-tuple-element.199, bf16[11008,2048]{1,0:T(8,128)(2,1)} %param.35, bf16[2048,11008]{1,0:T(8,128)(2,1)} %param.34, f32[64,11008]{1,0:T(8,128)} %fusion.61, f32[64]{0:T(128)S(1)} %add_rsqrt_fusion.1), kind=kOutput, calls=%fused_computation.119 | convolution fusion | flops 5777915904 | bytes 93782528 | tf_op jit(solution)/shard_map/dot_general | solution.py:45
  335.0 5.1 fusion.97
  342.2 3.2 copy-done.2
  349.0 25.6 %all_gather.15 = bf16[512,2,128]{2,0,1:T(8,128)(2,1)S(1)} all-gather(bf16[64,2,128]{2,0,1:T(8,128)(2,1)S(1)} %pad_maximum_fusion.3), channel_id=1, replica_groups=mesh['dp'=2,'cp'=8] {'cp'}, dimensions={0}, use_global_device_ids=true | all-gather | bytes 294912 | tf_op jit(solution)/shard_map/all_gather | solution.py:74
  377.6 22.7 %all_gather.14 = bf16[512,2,128]{2,0,1:T(8,128)(2,1)S(1)} all-gather(bf16[64,2,128]{2,0,1:T(8,128)(2,1)S(1)} %copy_bitcast_fusion), channel_id=1, replica_groups=mesh['dp'=2,'cp'=8] {'cp'}, dimensions={0}, use_global_device_ids=true | all-gather | bytes 294912 | tf_op jit(solution)/shard_map/all_gather | solution.py:75
  400.3 5.1 fusion.69
  409.2 205.6 %while.33 = (s32[]{:T(128)}, bf16[2048,2,128]{2,0,1:T(8,128)(2,1)}, bf16[2048,2,128]{2,0,1:T(8,128)(2,1)}, f32[64,2,8,128]{3,0,2,1:T(8,128)S(1)}, f32[64,2,8]{0,...) while((s32[]{:T(128)}, bf16[2048,2,128]{2,0,1:T(8,128)(2,1)}, ...), condition=%wide.region_17.18_spmd, body=%wide.region_14.17_spmd.sunk | while | flops 1091053568 | bytes 41222300 | solution.py:91
  409.2 5.3 collective-permute-start.2
  414.5 11.7 %collective-permute-done.2 = bf16[2048,2,128]{2,0,1:T(8,128)(2,1)S(1)} collective-permute-done((bf16[2048,2,128]{2,0,1:T(8,128)(2,1)}, bf16[2048,2,128]{2,0,1:T(8,128)(2,1)S(1)}, u32[]{:S(2)}, u32[]{:S(2)}) %collective-permute-start.2) | collective-permute-done | bytes 1048608 | tf_op jit(solution)/shard_map/while/body/eval_jaxpr/ppermute | solution.py:85
  430.2 7.2 %collective-permute-done.3 = bf16[2048,2,128]{2,0,1:T(8,128)(2,1)S(1)} collective-permute-done((bf16[2048,2,128]{2,0,1:T(8,128)(2,1)}, bf16[2048,2,128]{2,0,1:T(8,128)(2,1)S(1)}, u32[]{:S(2)}, u32[]{:S(2)}) %collective-permute-start.3) | collective-permute-done | bytes 1048608 | tf_op jit(solution)/shard_map/while/body/eval_jaxpr/ppermute | solution.py:86
  440.9 2.6 collective-permute-start.2
  443.5 11.7 %collective-permute-done.2 = bf16[2048,2,128]{2,0,1:T(8,128)(2,1)S(1)} collective-permute-done((bf16[2048,2,128]{2,0,1:T(8,128)(2,1)}, bf16[2048,2,128]{2,0,1:T(8,128)(2,1)S(1)}, u32[]{:S(2)}, u32[]{:S(2)}) %collective-permute-start.2) | collective-permute-done | bytes 1048608 | tf_op jit(solution)/shard_map/while/body/eval_jaxpr/ppermute | solution.py:85
  459.2 7.2 %collective-permute-done.3 = bf16[2048,2,128]{2,0,1:T(8,128)(2,1)S(1)} collective-permute-done((bf16[2048,2,128]{2,0,1:T(8,128)(2,1)}, bf16[2048,2,128]{2,0,1:T(8,128)(2,1)S(1)}, u32[]{:S(2)}, u32[]{:S(2)}) %collective-permute-start.3) | collective-permute-done | bytes 1048608 | tf_op jit(solution)/shard_map/while/body/eval_jaxpr/ppermute | solution.py:86
  467.4 2.4 fusion.185
  469.8 2.6 collective-permute-start.2
  472.5 11.7 %collective-permute-done.2 = bf16[2048,2,128]{2,0,1:T(8,128)(2,1)S(1)} collective-permute-done((bf16[2048,2,128]{2,0,1:T(8,128)(2,1)}, bf16[2048,2,128]{2,0,1:T(8,128)(2,1)S(1)}, u32[]{:S(2)}, u32[]{:S(2)}) %collective-permute-start.2) | collective-permute-done | bytes 1048608 | tf_op jit(solution)/shard_map/while/body/eval_jaxpr/ppermute | solution.py:85
  488.2 7.2 %collective-permute-done.3 = bf16[2048,2,128]{2,0,1:T(8,128)(2,1)S(1)} collective-permute-done((bf16[2048,2,128]{2,0,1:T(8,128)(2,1)}, bf16[2048,2,128]{2,0,1:T(8,128)(2,1)S(1)}, u32[]{:S(2)}, u32[]{:S(2)}) %collective-permute-start.3) | collective-permute-done | bytes 1048608 | tf_op jit(solution)/shard_map/while/body/eval_jaxpr/ppermute | solution.py:86
  496.4 2.4 fusion.185
  498.8 2.6 collective-permute-start.2
  501.5 11.7 %collective-permute-done.2 = bf16[2048,2,128]{2,0,1:T(8,128)(2,1)S(1)} collective-permute-done((bf16[2048,2,128]{2,0,1:T(8,128)(2,1)}, bf16[2048,2,128]{2,0,1:T(8,128)(2,1)S(1)}, u32[]{:S(2)}, u32[]{:S(2)}) %collective-permute-start.2) | collective-permute-done | bytes 1048608 | tf_op jit(solution)/shard_map/while/body/eval_jaxpr/ppermute | solution.py:85
  517.1 7.2 %collective-permute-done.3 = bf16[2048,2,128]{2,0,1:T(8,128)(2,1)S(1)} collective-permute-done((bf16[2048,2,128]{2,0,1:T(8,128)(2,1)}, bf16[2048,2,128]{2,0,1:T(8,128)(2,1)S(1)}, u32[]{:S(2)}, u32[]{:S(2)}) %collective-permute-start.3) | collective-permute-done | bytes 1048608 | tf_op jit(solution)/shard_map/while/body/eval_jaxpr/ppermute | solution.py:86
  525.4 2.4 fusion.185
  527.8 2.6 collective-permute-start.2
  530.4 11.7 %collective-permute-done.2 = bf16[2048,2,128]{2,0,1:T(8,128)(2,1)S(1)} collective-permute-done((bf16[2048,2,128]{2,0,1:T(8,128)(2,1)}, bf16[2048,2,128]{2,0,1:T(8,128)(2,1)S(1)}, u32[]{:S(2)}, u32[]{:S(2)}) %collective-permute-start.2) | collective-permute-done | bytes 1048608 | tf_op jit(solution)/shard_map/while/body/eval_jaxpr/ppermute | solution.py:85
  546.1 7.2 %collective-permute-done.3 = bf16[2048,2,128]{2,0,1:T(8,128)(2,1)S(1)} collective-permute-done((bf16[2048,2,128]{2,0,1:T(8,128)(2,1)}, bf16[2048,2,128]{2,0,1:T(8,128)(2,1)S(1)}, u32[]{:S(2)}, u32[]{:S(2)}) %collective-permute-start.3) | collective-permute-done | bytes 1048608 | tf_op jit(solution)/shard_map/while/body/eval_jaxpr/ppermute | solution.py:86
  554.3 2.4 fusion.185
  556.8 2.6 collective-permute-start.2
  559.4 11.7 %collective-permute-done.2 = bf16[2048,2,128]{2,0,1:T(8,128)(2,1)S(1)} collective-permute-done((bf16[2048,2,128]{2,0,1:T(8,128)(2,1)}, bf16[2048,2,128]{2,0,1:T(8,128)(2,1)S(1)}, u32[]{:S(2)}, u32[]{:S(2)}) %collective-permute-start.2) | collective-permute-done | bytes 1048608 | tf_op jit(solution)/shard_map/while/body/eval_jaxpr/ppermute | solution.py:85
  575.1 7.2 %collective-permute-done.3 = bf16[2048,2,128]{2,0,1:T(8,128)(2,1)S(1)} collective-permute-done((bf16[2048,2,128]{2,0,1:T(8,128)(2,1)}, bf16[2048,2,128]{2,0,1:T(8,128)(2,1)S(1)}, u32[]{:S(2)}, u32[]{:S(2)}) %collective-permute-start.3) | collective-permute-done | bytes 1048608 | tf_op jit(solution)/shard_map/while/body/eval_jaxpr/ppermute | solution.py:86
  583.3 2.4 fusion.185
  585.8 2.6 collective-permute-start.2
  588.4 11.7 %collective-permute-done.2 = bf16[2048,2,128]{2,0,1:T(8,128)(2,1)S(1)} collective-permute-done((bf16[2048,2,128]{2,0,1:T(8,128)(2,1)}, bf16[2048,2,128]{2,0,1:T(8,128)(2,1)S(1)}, u32[]{:S(2)}, u32[]{:S(2)}) %collective-permute-start.2) | collective-permute-done | bytes 1048608 | tf_op jit(solution)/shard_map/while/body/eval_jaxpr/ppermute | solution.py:85
  604.1 7.2 %collective-permute-done.3 = bf16[2048,2,128]{2,0,1:T(8,128)(2,1)S(1)} collective-permute-done((bf16[2048,2,128]{2,0,1:T(8,128)(2,1)}, bf16[2048,2,128]{2,0,1:T(8,128)(2,1)S(1)}, u32[]{:S(2)}, u32[]{:S(2)}) %collective-permute-start.3) | collective-permute-done | bytes 1048608 | tf_op jit(solution)/shard_map/while/body/eval_jaxpr/ppermute | solution.py:86
  612.3 2.4 fusion.185
  615.0 5.7 convolution_convert_fusion.2
  (209 shorter events, 121.7 us)
Async XLA Ops:
  0.6 1.2 copy-start
  3.4 19.9 %copy-start.14 = (bf16[64,2,128]{2,0,1:T(8,128)(2,1)}, bf16[64,2,128]{2,0,1:T(8,128)(2,1)S(1)}, u32[]{:S(2)}) copy-start(bf16[64,2,128]{2,0,1:T(8,128)(2,1)S(1)} %pad_maximum_fusion.2) | copy-start | bytes 98308
  28.4 2.7 copy-start.9
  29.7 1.4 copy-start.4
  32.4 3.2 copy-start.3
  35.6 6.9 %copy-start.8 = (bf16[64,2048]{1,0:T(8,128)(2,1)S(1)}, bf16[64,2048]{1,0:T(8,128)(2,1)}, u32[]{:S(2)}) copy-start(bf16[64,2048]{1,0:T(8,128)(2,1)} %param.24) | copy-start | bytes 786436
  35.6 6.9 %copy-start.12 = (bf16[2048,256]{1,0:T(8,128)(2,1)S(1)}, bf16[2048,256]{1,0:T(8,128)(2,1)}, u32[]{:S(2)}) copy-start(bf16[2048,256]{1,0:T(8,128)(2,1)} %param.31) | copy-start | bytes 3145732
  42.8 0.6 copy-start.16
  70.8 18.6 %collective-permute-start = (bf16[2048,2,128]{2,0,1:T(8,128)(2,1)}, bf16[2048,2,128]{2,0,1:T(8,128)(2,1)S(1)}, u32[]{:S(2)}, u32[]{:S(2)}) collective-permute-start(bf16[2048,2,128]{2,0,1:T(8,128)(2,1)} %get-tuple-element.304), channel_id=1, source_target_pairs={{0,1},{1,2},{2,3},{3,4},{4,5},{5,6},{6,7},{7,0},{8,9},{9,10},{10,1... | collective-permute-start | bytes 3145736 | tf_op jit(solution)/shard_map/while/body/eval_jaxpr/ppermute | solution.py:85
  77.6 23.0 %collective-permute-start.1 = (bf16[2048,2,128]{2,0,1:T(8,128)(2,1)}, bf16[2048,2,128]{2,0,1:T(8,128)(2,1)S(1)}, u32[]{:S(2)}, u32[]{:S(2)}) collective-permute-start(bf16[2048,2,128]{2,0,1:T(8,128)(2,1)} %get-tuple-element.305), channel_id=1, source_target_pairs={{0,1},{1,2},{2,3},{3,4},{4,5},{5,6},{6,7},{7,0},{8,9},{9,10},{10,1... | collective-permute-start | bytes 3145736 | tf_op jit(solution)/shard_map/while/body/eval_jaxpr/ppermute | solution.py:86
  104.1 14.3 %collective-permute-start = (bf16[2048,2,128]{2,0,1:T(8,128)(2,1)}, bf16[2048,2,128]{2,0,1:T(8,128)(2,1)S(1)}, u32[]{:S(2)}, u32[]{:S(2)}) collective-permute-start(bf16[2048,2,128]{2,0,1:T(8,128)(2,1)} %get-tuple-element.304), channel_id=1, source_target_pairs={{0,1},{1,2},{2,3},{3,4},{4,5},{5,6},{6,7},{7,0},{8,9},{9,10},{10,1... | collective-permute-start | bytes 3145736 | tf_op jit(solution)/shard_map/while/body/eval_jaxpr/ppermute | solution.py:85
  106.6 23.0 %collective-permute-start.1 = (bf16[2048,2,128]{2,0,1:T(8,128)(2,1)}, bf16[2048,2,128]{2,0,1:T(8,128)(2,1)S(1)}, u32[]{:S(2)}, u32[]{:S(2)}) collective-permute-start(bf16[2048,2,128]{2,0,1:T(8,128)(2,1)} %get-tuple-element.305), channel_id=1, source_target_pairs={{0,1},{1,2},{2,3},{3,4},{4,5},{5,6},{6,7},{7,0},{8,9},{9,10},{10,1... | collective-permute-start | bytes 3145736 | tf_op jit(solution)/shard_map/while/body/eval_jaxpr/ppermute | solution.py:86
  133.0 14.3 %collective-permute-start = (bf16[2048,2,128]{2,0,1:T(8,128)(2,1)}, bf16[2048,2,128]{2,0,1:T(8,128)(2,1)S(1)}, u32[]{:S(2)}, u32[]{:S(2)}) collective-permute-start(bf16[2048,2,128]{2,0,1:T(8,128)(2,1)} %get-tuple-element.304), channel_id=1, source_target_pairs={{0,1},{1,2},{2,3},{3,4},{4,5},{5,6},{6,7},{7,0},{8,9},{9,10},{10,1... | collective-permute-start | bytes 3145736 | tf_op jit(solution)/shard_map/while/body/eval_jaxpr/ppermute | solution.py:85
  135.5 23.0 %collective-permute-start.1 = (bf16[2048,2,128]{2,0,1:T(8,128)(2,1)}, bf16[2048,2,128]{2,0,1:T(8,128)(2,1)S(1)}, u32[]{:S(2)}, u32[]{:S(2)}) collective-permute-start(bf16[2048,2,128]{2,0,1:T(8,128)(2,1)} %get-tuple-element.305), channel_id=1, source_target_pairs={{0,1},{1,2},{2,3},{3,4},{4,5},{5,6},{6,7},{7,0},{8,9},{9,10},{10,1... | collective-permute-start | bytes 3145736 | tf_op jit(solution)/shard_map/while/body/eval_jaxpr/ppermute | solution.py:86
  162.0 14.3 %collective-permute-start = (bf16[2048,2,128]{2,0,1:T(8,128)(2,1)}, bf16[2048,2,128]{2,0,1:T(8,128)(2,1)S(1)}, u32[]{:S(2)}, u32[]{:S(2)}) collective-permute-start(bf16[2048,2,128]{2,0,1:T(8,128)(2,1)} %get-tuple-element.304), channel_id=1, source_target_pairs={{0,1},{1,2},{2,3},{3,4},{4,5},{5,6},{6,7},{7,0},{8,9},{9,10},{10,1... | collective-permute-start | bytes 3145736 | tf_op jit(solution)/shard_map/while/body/eval_jaxpr/ppermute | solution.py:85
  164.5 23.0 %collective-permute-start.1 = (bf16[2048,2,128]{2,0,1:T(8,128)(2,1)}, bf16[2048,2,128]{2,0,1:T(8,128)(2,1)S(1)}, u32[]{:S(2)}, u32[]{:S(2)}) collective-permute-start(bf16[2048,2,128]{2,0,1:T(8,128)(2,1)} %get-tuple-element.305), channel_id=1, source_target_pairs={{0,1},{1,2},{2,3},{3,4},{4,5},{5,6},{6,7},{7,0},{8,9},{9,10},{10,1... | collective-permute-start | bytes 3145736 | tf_op jit(solution)/shard_map/while/body/eval_jaxpr/ppermute | solution.py:86
  190.9 14.3 %collective-permute-start = (bf16[2048,2,128]{2,0,1:T(8,128)(2,1)}, bf16[2048,2,128]{2,0,1:T(8,128)(2,1)S(1)}, u32[]{:S(2)}, u32[]{:S(2)}) collective-permute-start(bf16[2048,2,128]{2,0,1:T(8,128)(2,1)} %get-tuple-element.304), channel_id=1, source_target_pairs={{0,1},{1,2},{2,3},{3,4},{4,5},{5,6},{6,7},{7,0},{8,9},{9,10},{10,1... | collective-permute-start | bytes 3145736 | tf_op jit(solution)/shard_map/while/body/eval_jaxpr/ppermute | solution.py:85
  193.5 23.0 %collective-permute-start.1 = (bf16[2048,2,128]{2,0,1:T(8,128)(2,1)}, bf16[2048,2,128]{2,0,1:T(8,128)(2,1)S(1)}, u32[]{:S(2)}, u32[]{:S(2)}) collective-permute-start(bf16[2048,2,128]{2,0,1:T(8,128)(2,1)} %get-tuple-element.305), channel_id=1, source_target_pairs={{0,1},{1,2},{2,3},{3,4},{4,5},{5,6},{6,7},{7,0},{8,9},{9,10},{10,1... | collective-permute-start | bytes 3145736 | tf_op jit(solution)/shard_map/while/body/eval_jaxpr/ppermute | solution.py:86
  219.9 14.3 %collective-permute-start = (bf16[2048,2,128]{2,0,1:T(8,128)(2,1)}, bf16[2048,2,128]{2,0,1:T(8,128)(2,1)S(1)}, u32[]{:S(2)}, u32[]{:S(2)}) collective-permute-start(bf16[2048,2,128]{2,0,1:T(8,128)(2,1)} %get-tuple-element.304), channel_id=1, source_target_pairs={{0,1},{1,2},{2,3},{3,4},{4,5},{5,6},{6,7},{7,0},{8,9},{9,10},{10,1... | collective-permute-start | bytes 3145736 | tf_op jit(solution)/shard_map/while/body/eval_jaxpr/ppermute | solution.py:85
  222.4 23.0 %collective-permute-start.1 = (bf16[2048,2,128]{2,0,1:T(8,128)(2,1)}, bf16[2048,2,128]{2,0,1:T(8,128)(2,1)S(1)}, u32[]{:S(2)}, u32[]{:S(2)}) collective-permute-start(bf16[2048,2,128]{2,0,1:T(8,128)(2,1)} %get-tuple-element.305), channel_id=1, source_target_pairs={{0,1},{1,2},{2,3},{3,4},{4,5},{5,6},{6,7},{7,0},{8,9},{9,10},{10,1... | collective-permute-start | bytes 3145736 | tf_op jit(solution)/shard_map/while/body/eval_jaxpr/ppermute | solution.py:86
  248.9 14.3 %collective-permute-start = (bf16[2048,2,128]{2,0,1:T(8,128)(2,1)}, bf16[2048,2,128]{2,0,1:T(8,128)(2,1)S(1)}, u32[]{:S(2)}, u32[]{:S(2)}) collective-permute-start(bf16[2048,2,128]{2,0,1:T(8,128)(2,1)} %get-tuple-element.304), channel_id=1, source_target_pairs={{0,1},{1,2},{2,3},{3,4},{4,5},{5,6},{6,7},{7,0},{8,9},{9,10},{10,1... | collective-permute-start | bytes 3145736 | tf_op jit(solution)/shard_map/while/body/eval_jaxpr/ppermute | solution.py:85
  251.4 23.0 %collective-permute-start.1 = (bf16[2048,2,128]{2,0,1:T(8,128)(2,1)}, bf16[2048,2,128]{2,0,1:T(8,128)(2,1)S(1)}, u32[]{:S(2)}, u32[]{:S(2)}) collective-permute-start(bf16[2048,2,128]{2,0,1:T(8,128)(2,1)} %get-tuple-element.305), channel_id=1, source_target_pairs={{0,1},{1,2},{2,3},{3,4},{4,5},{5,6},{6,7},{7,0},{8,9},{9,10},{10,1... | collective-permute-start | bytes 3145736 | tf_op jit(solution)/shard_map/while/body/eval_jaxpr/ppermute | solution.py:86
  302.6 32.4 %copy-start.18 = (bf16[2048]{0:T(1024)(128)(2,1)S(1)}, bf16[2048]{0:T(1024)(128)(2,1)}, u32[]{:S(2)}) copy-start(bf16[2048]{0:T(1024)(128)(2,1)} %param.39) | copy-start | bytes 12292
  335.0 42.3 %copy-start.7 = (bf16[64,2048]{1,0:T(8,128)(2,1)}, bf16[64,2048]{1,0:T(8,128)(2,1)S(1)}, u32[]{:S(2)}) copy-start(bf16[64,2048]{1,0:T(8,128)(2,1)S(1)} %get-tuple-element.201) | copy-start | bytes 786436
  335.0 5.8 copy-start.10
  340.8 6.3 %copy-start.19 = (bf16[256]{0:T(256)(128)(2,1)S(1)}, bf16[256]{0:T(256)(128)(2,1)}, u32[]{:S(2)}) copy-start(bf16[256]{0:T(256)(128)(2,1)} %param.41) | copy-start | bytes 1540
  342.2 3.2 copy-start.2
  342.2 35.1 %copy-start.11 = (bf16[2048,256]{1,0:T(8,128)(2,1)S(1)}, bf16[2048,256]{1,0:T(8,128)(2,1)}, u32[]{:S(2)}) copy-start(bf16[2048,256]{1,0:T(8,128)(2,1)} %param.42) | copy-start | bytes 3145732
  375.1 1.4 copy-start.5
  377.2 28.2 %copy-start.6 = (f32[64,2,8,512]{3,0,2,1:T(8,128)S(1)}, f32[64,2,8,512]{3,0,2,1:T(8,128)}, u32[]{:S(2)}) copy-start(f32[64,2,8,512]{3,0,2,1:T(8,128)} %copy-done.5) | copy-start | bytes 6291460
  400.3 7.7 %copy-start.13 = (bf16[2048,2,128]{2,1,0:T(2,128)(2,1)S(1)}, bf16[2048,2,128]{2,1,0:T(2,128)(2,1)}, u32[]{:S(2)}) copy-start(bf16[2048,2,128]{2,1,0:T(2,128)(2,1)} %param.37) | copy-start | bytes 3145732
  409.2 17.0 %collective-permute-start.2 = (bf16[2048,2,128]{2,0,1:T(8,128)(2,1)}, bf16[2048,2,128]{2,0,1:T(8,128)(2,1)S(1)}, u32[]{:S(2)}, u32[]{:S(2)}) collective-permute-start(bf16[2048,2,128]{2,0,1:T(8,128)(2,1)} %get-tuple-element.325), channel_id=1, source_target_pairs={{0,1},{1,2},{2,3},{3,4},{4,5},{5,6},{6,7},{7,0},{8,9},{9,10},{10,1... | collective-permute-start | bytes 3145736 | tf_op jit(solution)/shard_map/while/body/eval_jaxpr/ppermute | solution.py:85
  414.4 23.0 %collective-permute-start.3 = (bf16[2048,2,128]{2,0,1:T(8,128)(2,1)}, bf16[2048,2,128]{2,0,1:T(8,128)(2,1)S(1)}, u32[]{:S(2)}, u32[]{:S(2)}) collective-permute-start(bf16[2048,2,128]{2,0,1:T(8,128)(2,1)} %get-tuple-element.326), channel_id=1, source_target_pairs={{0,1},{1,2},{2,3},{3,4},{4,5},{5,6},{6,7},{7,0},{8,9},{9,10},{10,1... | collective-permute-start | bytes 3145736 | tf_op jit(solution)/shard_map/while/body/eval_jaxpr/ppermute | solution.py:86
  440.9 14.3 %collective-permute-start.2 = (bf16[2048,2,128]{2,0,1:T(8,128)(2,1)}, bf16[2048,2,128]{2,0,1:T(8,128)(2,1)S(1)}, u32[]{:S(2)}, u32[]{:S(2)}) collective-permute-start(bf16[2048,2,128]{2,0,1:T(8,128)(2,1)} %get-tuple-element.325), channel_id=1, source_target_pairs={{0,1},{1,2},{2,3},{3,4},{4,5},{5,6},{6,7},{7,0},{8,9},{9,10},{10,1... | collective-permute-start | bytes 3145736 | tf_op jit(solution)/shard_map/while/body/eval_jaxpr/ppermute | solution.py:85
  443.4 23.0 %collective-permute-start.3 = (bf16[2048,2,128]{2,0,1:T(8,128)(2,1)}, bf16[2048,2,128]{2,0,1:T(8,128)(2,1)S(1)}, u32[]{:S(2)}, u32[]{:S(2)}) collective-permute-start(bf16[2048,2,128]{2,0,1:T(8,128)(2,1)} %get-tuple-element.326), channel_id=1, source_target_pairs={{0,1},{1,2},{2,3},{3,4},{4,5},{5,6},{6,7},{7,0},{8,9},{9,10},{10,1... | collective-permute-start | bytes 3145736 | tf_op jit(solution)/shard_map/while/body/eval_jaxpr/ppermute | solution.py:86
  469.8 14.3 %collective-permute-start.2 = (bf16[2048,2,128]{2,0,1:T(8,128)(2,1)}, bf16[2048,2,128]{2,0,1:T(8,128)(2,1)S(1)}, u32[]{:S(2)}, u32[]{:S(2)}) collective-permute-start(bf16[2048,2,128]{2,0,1:T(8,128)(2,1)} %get-tuple-element.325), channel_id=1, source_target_pairs={{0,1},{1,2},{2,3},{3,4},{4,5},{5,6},{6,7},{7,0},{8,9},{9,10},{10,1... | collective-permute-start | bytes 3145736 | tf_op jit(solution)/shard_map/while/body/eval_jaxpr/ppermute | solution.py:85
  472.4 23.0 %collective-permute-start.3 = (bf16[2048,2,128]{2,0,1:T(8,128)(2,1)}, bf16[2048,2,128]{2,0,1:T(8,128)(2,1)S(1)}, u32[]{:S(2)}, u32[]{:S(2)}) collective-permute-start(bf16[2048,2,128]{2,0,1:T(8,128)(2,1)} %get-tuple-element.326), channel_id=1, source_target_pairs={{0,1},{1,2},{2,3},{3,4},{4,5},{5,6},{6,7},{7,0},{8,9},{9,10},{10,1... | collective-permute-start | bytes 3145736 | tf_op jit(solution)/shard_map/while/body/eval_jaxpr/ppermute | solution.py:86
  498.8 14.3 %collective-permute-start.2 = (bf16[2048,2,128]{2,0,1:T(8,128)(2,1)}, bf16[2048,2,128]{2,0,1:T(8,128)(2,1)S(1)}, u32[]{:S(2)}, u32[]{:S(2)}) collective-permute-start(bf16[2048,2,128]{2,0,1:T(8,128)(2,1)} %get-tuple-element.325), channel_id=1, source_target_pairs={{0,1},{1,2},{2,3},{3,4},{4,5},{5,6},{6,7},{7,0},{8,9},{9,10},{10,1... | collective-permute-start | bytes 3145736 | tf_op jit(solution)/shard_map/while/body/eval_jaxpr/ppermute | solution.py:85
  501.4 23.0 %collective-permute-start.3 = (bf16[2048,2,128]{2,0,1:T(8,128)(2,1)}, bf16[2048,2,128]{2,0,1:T(8,128)(2,1)S(1)}, u32[]{:S(2)}, u32[]{:S(2)}) collective-permute-start(bf16[2048,2,128]{2,0,1:T(8,128)(2,1)} %get-tuple-element.326), channel_id=1, source_target_pairs={{0,1},{1,2},{2,3},{3,4},{4,5},{5,6},{6,7},{7,0},{8,9},{9,10},{10,1... | collective-permute-start | bytes 3145736 | tf_op jit(solution)/shard_map/while/body/eval_jaxpr/ppermute | solution.py:86
  527.8 14.3 %collective-permute-start.2 = (bf16[2048,2,128]{2,0,1:T(8,128)(2,1)}, bf16[2048,2,128]{2,0,1:T(8,128)(2,1)S(1)}, u32[]{:S(2)}, u32[]{:S(2)}) collective-permute-start(bf16[2048,2,128]{2,0,1:T(8,128)(2,1)} %get-tuple-element.325), channel_id=1, source_target_pairs={{0,1},{1,2},{2,3},{3,4},{4,5},{5,6},{6,7},{7,0},{8,9},{9,10},{10,1... | collective-permute-start | bytes 3145736 | tf_op jit(solution)/shard_map/while/body/eval_jaxpr/ppermute | solution.py:85
  530.4 23.0 %collective-permute-start.3 = (bf16[2048,2,128]{2,0,1:T(8,128)(2,1)}, bf16[2048,2,128]{2,0,1:T(8,128)(2,1)S(1)}, u32[]{:S(2)}, u32[]{:S(2)}) collective-permute-start(bf16[2048,2,128]{2,0,1:T(8,128)(2,1)} %get-tuple-element.326), channel_id=1, source_target_pairs={{0,1},{1,2},{2,3},{3,4},{4,5},{5,6},{6,7},{7,0},{8,9},{9,10},{10,1... | collective-permute-start | bytes 3145736 | tf_op jit(solution)/shard_map/while/body/eval_jaxpr/ppermute | solution.py:86
  556.8 14.3 %collective-permute-start.2 = (bf16[2048,2,128]{2,0,1:T(8,128)(2,1)}, bf16[2048,2,128]{2,0,1:T(8,128)(2,1)S(1)}, u32[]{:S(2)}, u32[]{:S(2)}) collective-permute-start(bf16[2048,2,128]{2,0,1:T(8,128)(2,1)} %get-tuple-element.325), channel_id=1, source_target_pairs={{0,1},{1,2},{2,3},{3,4},{4,5},{5,6},{6,7},{7,0},{8,9},{9,10},{10,1... | collective-permute-start | bytes 3145736 | tf_op jit(solution)/shard_map/while/body/eval_jaxpr/ppermute | solution.py:85
  559.4 23.0 %collective-permute-start.3 = (bf16[2048,2,128]{2,0,1:T(8,128)(2,1)}, bf16[2048,2,128]{2,0,1:T(8,128)(2,1)S(1)}, u32[]{:S(2)}, u32[]{:S(2)}) collective-permute-start(bf16[2048,2,128]{2,0,1:T(8,128)(2,1)} %get-tuple-element.326), channel_id=1, source_target_pairs={{0,1},{1,2},{2,3},{3,4},{4,5},{5,6},{6,7},{7,0},{8,9},{9,10},{10,1... | collective-permute-start | bytes 3145736 | tf_op jit(solution)/shard_map/while/body/eval_jaxpr/ppermute | solution.py:86
  585.8 14.3 %collective-permute-start.2 = (bf16[2048,2,128]{2,0,1:T(8,128)(2,1)}, bf16[2048,2,128]{2,0,1:T(8,128)(2,1)S(1)}, u32[]{:S(2)}, u32[]{:S(2)}) collective-permute-start(bf16[2048,2,128]{2,0,1:T(8,128)(2,1)} %get-tuple-element.325), channel_id=1, source_target_pairs={{0,1},{1,2},{2,3},{3,4},{4,5},{5,6},{6,7},{7,0},{8,9},{9,10},{10,1... | collective-permute-start | bytes 3145736 | tf_op jit(solution)/shard_map/while/body/eval_jaxpr/ppermute | solution.py:85
  588.3 23.0 %collective-permute-start.3 = (bf16[2048,2,128]{2,0,1:T(8,128)(2,1)}, bf16[2048,2,128]{2,0,1:T(8,128)(2,1)S(1)}, u32[]{:S(2)}, u32[]{:S(2)}) collective-permute-start(bf16[2048,2,128]{2,0,1:T(8,128)(2,1)} %get-tuple-element.326), channel_id=1, source_target_pairs={{0,1},{1,2},{2,3},{3,4},{4,5},{5,6},{6,7},{7,0},{8,9},{9,10},{10,1... | collective-permute-start | bytes 3145736 | tf_op jit(solution)/shard_map/while/body/eval_jaxpr/ppermute | solution.py:86
  614.8 8.5 %copy-start.1 = (bf16[2048,256]{1,0:T(8,128)(2,1)S(1)}, bf16[2048,256]{1,0:T(8,128)(2,1)}, u32[]{:S(2)}) copy-start(bf16[2048,256]{1,0:T(8,128)(2,1)} %param.29) | copy-start | bytes 3145732
  615.0 7.0 %copy-start.15 = (bf16[64,2,128]{2,0,1:T(8,128)(2,1)S(1)}, bf16[64,2,128]{2,0,1:T(8,128)(2,1)}, u32[]{:S(2)}) copy-start(bf16[64,2,128]{2,0,1:T(8,128)(2,1)} %copy-done.14) | copy-start | bytes 98308
  615.0 7.7 %copy-start.17 = (bf16[64,256]{1,0:T(8,128)(2,1)S(1)}, bf16[64,256]{1,0:T(8,128)(2,1)}, u32[]{:S(2)}) copy-start(bf16[64,256]{1,0:T(8,128)(2,1)} %copy-done.16) | copy-start | bytes 98308
where the time goes:
time: 635 us; the launch traced here: 623 us
  waiting for transfers between devices  264 us (42%)
  matrix products  146 us (23%)
  blocking collectives  89.2 us (14%)
  local copies, waits for them, and re-layouts  46.9 us (7%)
  starting transfers between devices  43.6 us (7%)
  other arithmetic  31.5 us (5%)
    ppermute x14, waiting for transfers between devices, cache_step(): blk_k = lax.ppermute(blk_k, 'cp', shift)  163 us
    ppermute x14, waiting for transfers between devices, cache_step(): blk_v = lax.ppermute(blk_v, 'cp', shift)  101 us
    dot_general x18, matrix products, partial_attend(): jnp.einsum('tkgs,skd->tkgd', prob_w.astype(jnp.bfloat16), values, preferr...  47.7 us
    all_gather x2, blocking collectives, attention_layer(): all_k = lax.all_gather(k_new, 'cp', axis=0, tiled=True)  44.8 us
    all_gather x2, blocking collectives, attention_layer(): all_v = lax.all_gather(v_new, 'cp', axis=0, tiled=True)  44.4 us
    ppermute x14, starting transfers between devices, cache_step(): blk_k = lax.ppermute(blk_k, 'cp', shift)  42.7 us
    dot_general x1, matrix products, mlp_block(): jnp.dot(mixed, w_down, preferred_element_type=jnp.float32)  32.3 us
    reduce_sum x18, other arithmetic, partial_attend(): total = jnp.sum(prob_w, axis=-1)  27.8 us
  transfers between devices with their start and end apart: 28, of which 28 were waited for; matrix products, arithmetic and copies ran while one was open for 9% of the time, Pallas kernels for 0%

commit v1 on v0

v1 whole, which is shorter than its diff:
```python
import functools
import math

import jax
import jax.numpy as jnp
import numpy as np
from jax import lax
from jax.experimental import pallas as pl
from jax.experimental.pallas import tpu as pltpu
from jax.sharding import PartitionSpec as P

ROPE_THETA = 500000.0
NORM_EPS = 1e-5
MESH = pl.DeviceIdType.MESH
F32 = jnp.float32
BF16 = jnp.bfloat16

ORDER = ("own0", "own1", "own2", "left0", "right1", "opp0", "opp1", "left2", "right3", "opp2", "opp3",
         "right0", "left1", "right2", "left3", "own3")
SLOT = {name: idx for idx, name in enumerate(ORDER)}
UNITS = len(ORDER)
PAIRS = 4
NORM_ROWS = 16


def rope_tables(first_pos, count, head_dim):
    half_dim = head_dim // 2
    exponent = np.arange(half_dim, dtype=np.float32) * np.float32(2.0 / head_dim)
    inv_freq = (np.float32(1.0) / np.power(np.float32(ROPE_THETA), exponent)).astype(np.float32)
    positions = (first_pos + np.arange(count)).astype(np.float32)
    angles = (positions[:, None] * inv_freq[None, :]).astype(np.float32)
    cos_t = np.cos(angles.astype(np.float64)).astype(np.float32)
    sin_t = np.sin(angles.astype(np.float64)).astype(np.float32)
    return np.concatenate([cos_t, cos_t], axis=1), np.concatenate([-sin_t, sin_t], axis=1)


def block_kernel(nchip, ff_chunk, ff_slots,
                 x_hbm, kc1, vc1, wq1, wk1, wv1, wo1, w_gate, w_up, w_down, kc2, vc2, wq2, wk2, wv2, wo2,
                 bias_ref, cos_hbm, sin_hbm,
                 g_out, y_out, k1_out, v1_out, k2_out, v2_out,
                 xbuf, hbuf, ubuf, wqb, wkb, wvb, wob, kall, vtall, kstage, vstage, ksend, vsend, deint,
                 qall, s_a, s_b, m_a, m_b, obuf, relay, final, ohalf, ysend, yrecv, macc, mrecv,
                 w1s, w3s, w2s, ebuf, cosb, sinb, kvout, gout,
                 dsem, rings, ssem, rsem):
    tok = x_hbm.shape[0]
    ctok = 2 * tok
    width = x_hbm.shape[1]
    hd = kc1.shape[1]
    keys_dev = kc1.shape[0] // 2
    keys_chip = 2 * keys_dev
    keys_tot = keys_chip + ctok
    rows = 2 * ctok
    half_w = width // 2
    ncol = 4
    cw = width // ncol
    cexp = math.log2(math.e) / math.sqrt(hd)

    me = lax.axis_index("cp")
    chip = me // 2
    core = lax.rem(me, 2)
    partner = chip * 2 + 1 - core
    left_chip = lax.rem(chip + nchip - 1, nchip)
    right_chip = lax.rem(chip + 1, nchip)
    opp_chip = lax.rem(chip + 2, nchip)
    left = left_chip * 2 + core
    right = right_chip * 2 + core

    dcount = [0]

    def local(src, dst):
        idx = dcount[0]
        dcount[0] += 1
        return pltpu.make_async_copy(src, dst, dsem.at[idx])

    rcount = [0]

    def remote(src, dst, dev):
        idx = rcount[0]
        rcount[0] += 1
        return pltpu.make_async_remote_copy(src_ref=src, dst_ref=dst, send_sem=ssem.at[idx], recv_sem=rsem.at[idx],
                                            device_id={"cp": dev}, device_id_type=MESH)

    barrier = pltpu.get_barrier_semaphore()
    for dev in (partner, left, right):
        pl.semaphore_signal(barrier, inc=1, device_id={"cp": dev}, device_id_type=MESH)

    my_rows = pl.ds(pl.multiple_of(core * tok, tok), tok)
    kc = (kc1, kc2)
    vc = (vc1, vc2)
    wq = (wq1, wq2)
    wk = (wk1, wk2)
    wv = (wv1, wv2)
    wo = (wo1, wo2)
    k_out = (k1_out, k2_out)
    v_out = (v1_out, v2_out)

    cp_x = local(x_hbm, xbuf.at[my_rows])
    pos_rows = pl.ds(pl.multiple_of(chip * ctok, ctok), ctok)
    cp_cos = local(cos_hbm.at[pos_rows], cosb)
    cp_sin = local(sin_hbm.at[pos_rows], sinb)
    cp_ks = [local(kc[la], kstage) for la in range(2)]
    cp_vs = [local(vc[la], vstage) for la in range(2)]
    qcol = [pl.ds(pl.multiple_of(core * half_w + hp * rows, rows), rows) for hp in range(PAIRS)]
    cp_wq = [[local(wq[la].at[:, qcol[hp]], wqb.at[hp]) for hp in range(PAIRS)] for la in range(2)]
    cp_wk = [local(wk[la], wkb) for la in range(2)]
    cp_wv = [local(wv[la], wvb) for la in range(2)]
    cp_wo = [local(wo[la].at[pl.ds(pl.multiple_of(core * half_w, half_w), half_w)], wob) for la in range(2)]
    cp_kout = [local(kvout.at[la, 0], k_out[la]) for la in range(2)]
    cp_vout = [local(kvout.at[la, 1], v_out[la]) for la in range(2)]
    cp_g = local(gout.at[0], g_out)
    cp_y = local(gout.at[1], y_out)

    rc_x = remote(x_hbm, xbuf.at[my_rows], partner)
    rc_k = [remote(ksend, kall.at[la, pl.ds(keys_dev, keys_dev)], partner) for la in range(2)]
    rc_v = [remote(vsend, vtall.at[la, :, pl.ds(keys_dev, keys_dev)], partner) for la in range(2)]
    rc_qr, rc_ql, rc_qf, rc_o = [], [], [], []
    for la in range(2):
        own = [qall.at[la, SLOT["own%d" % hp]] for hp in range(PAIRS)]
        rc_qr.append([remote(own[hp], qall.at[la, SLOT["left%d" % hp]], right) for hp in range(PAIRS)])
        rc_ql.append([remote(own[hp], qall.at[la, SLOT["right%d" % hp]], left) for hp in range(PAIRS)])
        fwd = []
        for hp in range(PAIRS):
            side, dev = ("left", right) if hp % 2 == 0 else ("right", left)
            fwd.append(remote(qall.at[la, SLOT["%s%d" % (side, hp)]], qall.at[la, SLOT["opp%d" % hp]], dev))
        rc_qf.append(fwd)
        outs = {}
        for hp in range(PAIRS):
            outs["left%d" % hp] = remote(obuf.at[SLOT["left%d" % hp]], final.at[la, 1, hp], left)
            outs["right%d" % hp] = remote(obuf.at[SLOT["right%d" % hp]], final.at[la, 0, hp], right)
            outs["opp%d" % hp] = remote(obuf.at[SLOT["opp%d" % hp]], relay.at[la, hp], right if hp % 2 == 0 else left)
        rc_o.append(outs)
    rc_y1 = [remote(ysend.at[n], yrecv.at[n], partner) for n in range(ncol)]
    other_rows = pl.ds(pl.multiple_of((1 - core) * tok, tok), tok)
    rc_y2 = [remote(ysend.at[n, other_rows], mrecv.at[n, pl.ds(ctok, tok)], partner) for n in range(ncol)]
    rc_m = [remote(macc.at[n], mrecv.at[n, pl.ds(0, ctok)], partner) for n in range(ncol)]

    ff_half = w_gate.shape[1] // 2
    nfull = ff_half // ff_chunk
    tail = ff_half - nfull * ff_chunk

    def ff_copies(chunk, slot, size):
        cols = pl.ds(pl.multiple_of(core * ff_half + chunk * ff_chunk, 128), size)
        return (pltpu.make_async_copy(w_gate.at[:, cols], w1s.at[slot, :, pl.ds(0, size)], rings.at[0, slot]),
                pltpu.make_async_copy(w_up.at[:, cols], w3s.at[slot, :, pl.ds(0, size)], rings.at[1, slot]),
                pltpu.make_async_copy(w_down.at[cols], w2s.at[slot, pl.ds(0, size)], rings.at[2, slot]))

    def rope(val, la_bias, cos_v, sin_v):
        val = (val + la_bias).astype(BF16).astype(F32)
        return (val * cos_v + pltpu.roll(val, hd // 2, 1) * sin_v).astype(BF16)

    def prep_cache(la):
        if la == 1:
            rc_k[0].wait_send()
            rc_v[0].wait_send()
        step_rows = 2 * hd

        def split(ref, i):
            deint[...] = ref[pl.ds(pl.multiple_of(i * step_rows, step_rows), step_rows), :].astype(F32)
            head0 = deint[pl.ds(0, hd, stride=2), :]
            head1 = deint[pl.ds(1, hd, stride=2), :]
            is0 = core == 0
            return jnp.where(is0, head0, head1), jnp.where(is0, head1, head0)

        def kbody(i, _):
            mine, other = split(kstage, i)
            at = pl.ds(pl.multiple_of(i * hd, hd), hd)
            kall[la, at, :] = mine.astype(BF16)
            ksend[at, :] = other.astype(BF16)
            return 0

        def vbody(i, _):
            mine, other = split(vstage, i)
            at = pl.ds(pl.multiple_of(i * hd, hd), hd)
            vtall[la, :, at] = mine.T.astype(BF16)
            vsend[:, at] = other.T.astype(BF16)
            return 0

        cp_ks[la].wait()
        lax.fori_loop(0, keys_dev // hd, kbody, 0)
        rc_k[la].start()
        cp_vs[la].wait()
        lax.fori_loop(0, keys_dev // hd, vbody, 0)
        rc_v[la].start()
        if la == 0:
            cp_ks[1].start()
            cp_vs[1].start()

    def project(la, in_ref):
        heads_all = wq1.shape[1] // hd
        base = la * (heads_all + 2)

        def bias_row(idx):
            return bias_ref[pl.ds(idx, 1), :]

        cos_v, sin_v = cosb[...], sinb[...]
        for hp in range(PAIRS):
            cp_wq[la][hp].wait()
            acc = jnp.dot(in_ref[...], wqb[hp], preferred_element_type=F32)
            slot = SLOT["own%d" % hp]
            for j in range(2):
                row = base + core * (heads_all // 2) + hp * 2 + j
                qall[la, slot, pl.ds(j * ctok, ctok), :] = rope(acc[:, j * hd:(j + 1) * hd], bias_row(row), cos_v, sin_v)
            rc_qr[la][hp].start()
            rc_ql[la][hp].start()
        cp_wk[la].wait()
        acc = jnp.dot(in_ref[...], wkb[...], preferred_element_type=F32)
        k_heads = [rope(acc[:, j * hd:(j + 1) * hd], bias_row(base + heads_all + j), cos_v, sin_v).astype(F32) for j in range(2)]
        cp_wv[la].wait()
        acc = jnp.dot(in_ref[...], wvb[...], preferred_element_type=F32)
        v_heads = [acc[:, j * hd:(j + 1) * hd].astype(BF16).astype(F32) for j in range(2)]
        is0 = core == 0
        kall[la, pl.ds(keys_chip, ctok), :] = jnp.where(is0, k_heads[0], k_heads[1]).astype(BF16)
        vtall[la, :, pl.ds(keys_chip, ctok)] = jnp.where(is0, v_heads[0], v_heads[1]).T.astype(BF16)
        for which, heads in ((0, k_heads), (1, v_heads)):
            for j in range(2):
                mine = jnp.where(is0, heads[j][:tok], heads[j][tok:])
                deint[pl.ds(j, tok, stride=2), :] = mine
            kvout[la, which] = deint[pl.ds(0, 2 * tok), :].astype(BF16)
        cp_kout[la].start()
        cp_vout[la].start()

    offs = {"own": 0, "left": (left_chip - chip) * ctok, "right": (right_chip - chip) * ctok, "opp": (opp_chip - chip) * ctok}

    def unit_offset(unit):
        res = jnp.int32(0)
        for name, idx in SLOT.items():
            if not name.startswith("own"):
                res = jnp.where(unit == idx, offs[name[:-1]], res)
        return res

    def scores(la, unit, s_ref, m_ref):
        s_val = lax.dot_general(kall[la], qall[la, unit], (((1,), (1,)), ((), ())), preferred_element_type=F32)
        s_ref[pl.ds(0, keys_chip), :] = s_val[:keys_chip]
        peak = jnp.max(s_val[:keys_chip].reshape(keys_chip // 8, 8, rows), axis=0)
        key_i = lax.broadcasted_iota(jnp.int32, (ctok, rows), 0)
        tok_i = lax.broadcasted_iota(jnp.int32, (ctok, rows), 1) % ctok
        masked = jnp.where(key_i - tok_i <= unit_offset(unit), s_val[keys_chip:], -jnp.inf)
        s_ref[pl.ds(keys_chip, ctok), :] = masked
        m_ref[...] = jnp.maximum(peak, jnp.max(masked.reshape(ctok // 8, 8, rows), axis=0))

    row8 = lax.broadcasted_iota(jnp.int32, (8, rows), 0)

    def put(dst, out_v, peak, total):
        dst[pl.ds(0, hd), :] = out_v
        dst[pl.ds(hd, 8), :] = jnp.where(row8 == 0, peak, total)

    def get(src):
        return src[pl.ds(0, hd), :], src[pl.ds(hd, 1), :], src[pl.ds(hd + 1, 1), :]

    def merged(parts):
        peak = functools.reduce(jnp.maximum, [part[1] for part in parts])
        scales = [jnp.exp2((part[1] - peak) * cexp) for part in parts]
        out_v = functools.reduce(jnp.add, [part[0] * sc for part, sc in zip(parts, scales)])
        total = functools.reduce(jnp.add, [part[2] * sc for part, sc in zip(parts, scales)])
        return out_v, peak, total

    def attend_unit(la, unit, nxt, s_cur, m_cur, s_nxt, m_nxt):
        peak = jnp.max(m_cur[...], axis=0, keepdims=True)
        shift = jnp.broadcast_to(peak * cexp, (8, rows))
        prob = jnp.exp2(s_cur[...].reshape(keys_tot // 8, 8, rows) * cexp - shift[None])
        total = jnp.sum(jnp.sum(prob, axis=0), axis=0, keepdims=True)
        out_v = jnp.dot(vtall[la], prob.reshape(keys_tot, rows).astype(BF16), preferred_element_type=F32)
        scores(la, nxt, s_nxt, m_nxt)
        put(obuf.at[unit], out_v, peak, total)

    def before(la):
        acts = {}

        def add(name, *fns):
            acts.setdefault(SLOT[name] - 1, []).extend(fns)

        for hp in range(PAIRS):
            lw, rw = rc_qr[la][hp].wait_recv, rc_ql[la][hp].wait_recv
            fwd = rc_qf[la][hp]
            if hp % 2 == 0:
                acts.setdefault(2 if hp == 0 else 4, []).extend([lw, fwd.start])
                add("right%d" % hp, rw)
            else:
                acts.setdefault(3 if hp == 1 else 5, []).extend([rw, fwd.start])
                add("left%d" % hp, lw)
        for hp in range(PAIRS):
            add("opp%d" % hp, rc_qf[la][hp].wait_recv)
        return acts

    def after(la):
        acts = {}
        for name, cp in rc_o[la].items():
            hp = int(name[-1])
            merge_it = (name.startswith("right") and hp % 2 == 0) or (name.startswith("left") and hp % 2 == 1)

            def act(name=name, cp=cp, hp=hp, merge_it=merge_it):
                if merge_it:
                    rc_o[la]["opp%d" % hp].wait_recv()
                    put(obuf.at[SLOT[name]], *merged([get(obuf.at[SLOT[name]]), get(relay.at[la, hp])]))
                cp.start()

            acts[SLOT[name]] = [act]
        return acts

    def attention(la):
        rc_k[la].wait_recv()
        rc_v[la].wait_recv()
        scores(la, 0, s_a, m_a)
        pre, post = before(la), after(la)

        def run(acts, pair, parity):
            for unit, fns in acts.items():
                if unit % 2 == parity:
                    @pl.when(pair == unit // 2)
                    def _(fns=fns):
                        for fn in fns:
                            fn()

        def body(pair, _):
            run(pre, pair, 0)
            attend_unit(la, 2 * pair, 2 * pair + 1, s_a, m_a, s_b, m_b)
            run(post, pair, 0)
            run(pre, pair, 1)
            attend_unit(la, 2 * pair + 1, jnp.minimum(2 * pair + 2, UNITS - 1), s_b, m_b, s_a, m_a)
            run(post, pair, 1)
            return 0

        lax.fori_loop(0, UNITS // 2, body, 0)

    def finish_attention(la):
        for hp in range(PAIRS):
            rc_o[la]["right%d" % hp].wait_recv()
            rc_o[la]["left%d" % hp].wait_recv()
            out_v, _, total = merged([get(obuf.at[SLOT["own%d" % hp]]), get(final.at[la, 0, hp]), get(final.at[la, 1, hp])])
            out_v = out_v / total
            for j in range(2):
                ohalf[:, pl.ds((2 * hp + j) * hd, hd)] = out_v[:, j * ctok:(j + 1) * ctok].T.astype(BF16)
        cp_wo[la].wait()
        rc_y = (rc_y1, rc_y2)[la]
        for n in range(ncol):
            ysend[n] = jnp.dot(ohalf[...], wob[:, n * cw:(n + 1) * cw], preferred_element_type=F32)
            rc_y[n].start()
        for cp in list(rc_qr[la]) + list(rc_ql[la]) + list(rc_qf[la]) + list(rc_o[la].values()):
            cp.wait_send()

    def normed(wide):
        return (wide * lax.rsqrt(jnp.mean(wide * wide, axis=-1, keepdims=True) + NORM_EPS)).astype(BF16)

    def row_loop(count, fn):
        def body(i, _):
            fn(pl.ds(pl.multiple_of(i * NORM_ROWS, NORM_ROWS), NORM_ROWS))
            return 0

        lax.fori_loop(0, count // NORM_ROWS, body, 0)

    cp_x.start()
    cp_cos.start()
    cp_sin.start()
    cp_ks[0].start()
    cp_vs[0].start()
    for hp in range(PAIRS):
        cp_wq[0][hp].start()
    cp_wk[0].start()
    cp_wv[0].start()
    pl.semaphore_wait(barrier, 3)
    rc_x.start()
    prep_cache(0)
    cp_cos.wait()
    cp_sin.wait()
    cp_x.wait()
    rc_x.wait_recv()
    project(0, xbuf)
    for hp in range(PAIRS):
        cp_wq[1][hp].start()
    cp_wk[1].start()
    cp_wv[1].start()
    cp_wo[0].start()
    for slot in range(ff_slots):
        for cp in ff_copies(slot, slot, ff_chunk):
            cp.start()
    attention(0)
    prep_cache(1)
    finish_attention(0)
    for n in range(ncol):
        rc_y1[n].wait()

    def first_norm(rs):
        parts = [(ysend[n, rs, :] + yrecv[n, rs, :]).astype(BF16).astype(F32) for n in range(ncol)]
        res = (xbuf[rs, :].astype(F32) + jnp.concatenate(parts, axis=1)).astype(BF16)
        hbuf[rs, :] = res
        ubuf[rs, :] = normed(res.astype(F32))

    row_loop(ctok, first_norm)
    cp_wo[1].start()

    def gate_up(slot, size):
        gate = jnp.dot(ubuf[...], w1s[slot, :, pl.ds(0, size)], preferred_element_type=F32).astype(BF16).astype(F32)
        up = jnp.dot(ubuf[...], w3s[slot, :, pl.ds(0, size)], preferred_element_type=F32).astype(BF16).astype(F32)
        return (jax.nn.silu(gate) * up).astype(BF16)

    def down(slot, size):
        for n in range(ncol):
            macc[n] += jnp.dot(ebuf[:, pl.ds(0, size)], w2s[slot, pl.ds(0, size), pl.ds(n * cw, cw)], preferred_element_type=F32)

    def refill(chunk, which):
        for size, cond in ((ff_chunk, chunk < nfull), (tail, chunk == nfull)):
            if size:
                @pl.when(cond)
                def _(size=size):
                    cps = ff_copies(chunk, lax.rem(chunk, ff_slots), size)
                    for w in which:
                        cps[w].start()

    macc[...] = jnp.zeros(macc.shape, F32)
    first = ff_copies(0, 0, ff_chunk)
    first[0].wait()
    first[1].wait()
    ebuf[...] = gate_up(0, ff_chunk)
    refill(jnp.int32(ff_slots), (0, 1))

    def mlp_body(k, _):
        slot, prev = lax.rem(k, ff_slots), lax.rem(k - 1, ff_slots)
        cps = ff_copies(k, slot, ff_chunk)
        cps[0].wait()
        cps[1].wait()
        ff_copies(k - 1, prev, ff_chunk)[2].wait()
        hidden = gate_up(slot, ff_chunk)
        down(prev, ff_chunk)
        ebuf[...] = hidden
        refill(k + ff_slots, (0, 1))
        refill(k - 1 + ff_slots, (2,))
        return 0

    lax.fori_loop(1, nfull, mlp_body, 0)
    last_slot = (nfull - 1) % ff_slots
    ff_copies(nfull - 1, last_slot, ff_chunk)[2].wait()
    if tail:
        slot = nfull % ff_slots
        cps = ff_copies(nfull, slot, tail)
        cps[0].wait()
        cps[1].wait()
        hidden = gate_up(slot, tail)
        down(last_slot, ff_chunk)
        ebuf[:, pl.ds(0, tail)] = hidden
        cps[2].wait()
        down(slot, tail)
    else:
        down(last_slot, ff_chunk)
    for n in range(ncol):
        rc_m[n].start()
    for n in range(ncol):
        rc_m[n].wait()

    def second_norm(rs):
        acc = jnp.concatenate([macc[n, rs, :] + mrecv[n, rs, :] for n in range(ncol)], axis=1)
        res = (hbuf[rs, :].astype(F32) + acc).astype(BF16)
        hbuf[rs, :] = res
        ubuf[rs, :] = normed(res.astype(F32))

    row_loop(ctok, second_norm)
    gout[0] = hbuf[my_rows, :]
    cp_g.start()

    project(1, ubuf)
    attention(1)
    finish_attention(1)
    for n in range(ncol):
        rc_y2[n].wait()
        gout[1, :, pl.ds(n * cw, cw)] = (ysend[n, my_rows, :] + mrecv[n, pl.ds(ctok, tok), :]).astype(BF16)
    cp_y.start()
    rc_x.wait_send()
    rc_k[1].wait_send()
    rc_v[1].wait_send()
    for cp in cp_kout + cp_vout + [cp_g, cp_y]:
        cp.wait()


def solution(mesh):
    axis_size = mesh.shape["cp"]
    nchip = axis_size // 2
    ff_chunk, ff_slots = 512, 3
    rows_spec = P(("dp", "cp"), None)
    cache_spec = P(("dp", "cp"), None, None)
    mat_spec = P(None, None)
    vec_spec = P(None)
    layer_specs = (cache_spec, cache_spec, mat_spec, vec_spec, mat_spec, vec_spec, mat_spec, mat_spec)
    in_specs = (rows_spec,) + layer_specs + (mat_spec, mat_spec, mat_spec) + layer_specs
    out_specs = (rows_spec, rows_spec, cache_spec, cache_spec, cache_spec, cache_spec)

    def forward(x_in, cache_k1, cache_v1, w_q1, b_q1, w_k1, b_k1, w_v1, w_o1, w_gate, w_up, w_down,
                cache_k2, cache_v2, w_q2, b_q2, w_k2, b_k2, w_v2, w_o2):
        tok, width = x_in.shape
        cache_dev, kv_heads, hd = cache_k1.shape
        ctok = 2 * tok
        rows = 2 * ctok
        keys_tot = 2 * cache_dev + ctok
        cos_t, sin_t = rope_tables(axis_size * cache_dev, axis_size * tok, hd)
        bias = jnp.concatenate([b_q1, b_k1, b_q2, b_k2]).astype(F32).reshape(-1, hd)
        flat = lambda arr: arr.reshape(-1, hd)
        half_w = width // 2
        ncol = 4
        hbm = pl.BlockSpec(memory_space=pl.ANY)
        vmem = pl.BlockSpec(memory_space=pltpu.VMEM)
        scratch = [
            pltpu.VMEM((ctok, width), BF16),
            pltpu.VMEM((ctok, width), BF16),
            pltpu.VMEM((ctok, width), BF16),
            pltpu.VMEM((PAIRS, width, rows), BF16),
            pltpu.VMEM(w_k1.shape, BF16),
            pltpu.VMEM(w_v1.shape, BF16),
            pltpu.VMEM((half_w, width), BF16),
            pltpu.VMEM((2, keys_tot, hd), BF16),
            pltpu.VMEM((2, hd, keys_tot), BF16),
            pltpu.VMEM((2 * cache_dev, hd), BF16),
            pltpu.VMEM((2 * cache_dev, hd), BF16),
            pltpu.VMEM((cache_dev, hd), BF16),
            pltpu.VMEM((hd, cache_dev), BF16),
            pltpu.VMEM((2 * hd, hd), F32),
            pltpu.VMEM((2, UNITS, rows, hd), BF16),
            pltpu.VMEM((keys_tot, rows), F32),
            pltpu.VMEM((keys_tot, rows), F32),
            pltpu.VMEM((8, rows), F32),
            pltpu.VMEM((8, rows), F32),
            pltpu.VMEM((UNITS, hd + 8, rows), F32),
            pltpu.VMEM((2, PAIRS, hd + 8, rows), F32),
            pltpu.VMEM((2, 2, PAIRS, hd + 8, rows), F32),
            pltpu.VMEM((ctok, half_w), BF16),
            pltpu.VMEM((ncol, ctok, width // ncol), F32),
            pltpu.VMEM((ncol, ctok, width // ncol), F32),
            pltpu.VMEM((ncol, ctok, width // ncol), F32),
            pltpu.VMEM((ncol, ctok + tok, width // ncol), F32),
            pltpu.VMEM((ff_slots, width, ff_chunk), BF16),
            pltpu.VMEM((ff_slots, width, ff_chunk), BF16),
            pltpu.VMEM((ff_slots, ff_chunk, width), BF16),
            pltpu.VMEM((ctok, ff_chunk), BF16),
            pltpu.VMEM((ctok, hd), F32),
            pltpu.VMEM((ctok, hd), F32),
            pltpu.VMEM((2, 2, 2 * tok, hd), BF16),
            pltpu.VMEM((2, tok, width), BF16),
            pltpu.SemaphoreType.DMA((29,)),
            pltpu.SemaphoreType.DMA((3, ff_slots)),
            pltpu.SemaphoreType.DMA((65,)),
            pltpu.SemaphoreType.DMA((65,)),
        ]
        act = jax.ShapeDtypeStruct((tok, width), BF16)
        app = jax.ShapeDtypeStruct((kv_heads * tok, hd), BF16)
        outs = pl.pallas_call(
            functools.partial(block_kernel, nchip, ff_chunk, ff_slots),
            out_shape=(act, act, app, app, app, app),
            in_specs=[hbm] * 16 + [vmem, hbm, hbm],
            out_specs=(hbm,) * 6,
            scratch_shapes=scratch,
            compiler_params=pltpu.CompilerParams(collective_id=0, has_side_effects=True, vmem_limit_bytes=67043328),
        )(x_in, flat(cache_k1), flat(cache_v1), w_q1, w_k1, w_v1, w_o1, w_gate, w_up, w_down,
          flat(cache_k2), flat(cache_v2), w_q2, w_k2, w_v2, w_o2, bias, jnp.asarray(cos_t), jnp.asarray(sin_t))
        hidden, y_two = outs[:2]
        appends = [arr.reshape(tok, kv_heads, hd) for arr in outs[2:]]
        return (hidden, y_two, *appends)

    return jax.shard_map(forward, mesh=mesh, in_specs=in_specs, out_specs=out_specs, check_vma=False)
```

time: 635 us -> 113 us (0.18); the launches traced: 623 us -> 113 us
  waiting for transfers between devices: 264 us -> 0 us
  matrix products: 146 us -> 0 us
  Pallas kernels: 0 us -> 102 us
  blocking collectives: 89.2 us -> 0 us
  starting transfers between devices: 43.6 us -> 0 us
  local copies, waits for them, and re-layouts: 46.9 us -> 8.92 us
  other arithmetic: 31.5 us -> 1.35 us
    ppermute x28 -> x0, waiting for transfers between devices: 264 us -> none  [the longest x14 163 us: cache_step(): blk_k = lax.ppermute(blk_k, 'cp', shift)]
    dot_general x46 -> x0, matrix products: 146 us -> none  [the longest x18 47.7 us: partial_attend(): jnp.einsum('tkgs,skd->tkgd', prob_w.astype(jnp.bfloat16), values, preferr...]
    pallas_call x0 -> x1, Pallas kernels: none -> 102 us  [forward(): pl.pallas_call(functools.partial(block_kernel, nchip, ff_chunk, ff_slots)...]
    all_gather x4 -> x0, blocking collectives: 89.2 us -> none  [the longest x2 44.8 us: attention_layer(): all_k = lax.all_gather(k_new, 'cp', axis=0, tiled=True)]
    ppermute x28 -> x0, starting transfers between devices: 43.6 us -> none  [the longest x14 42.7 us: cache_step(): blk_k = lax.ppermute(blk_k, 'cp', shift)]
    while x32 -> x0, local copies, waits for them, and re-layouts: 33.5 us -> none
    reduce_sum x18 -> x0, other arithmetic: 27.8 us -> none  [partial_attend(): total = jnp.sum(prob_w, axis=-1)]
  transfers between devices with their start and end apart: 28 -> 0, of which waited for: 28 -> 0; matrix products, arithmetic and copies ran while one was open for 9% -> 0% of each run, Pallas kernels for 0% -> 0%
where the time goes in v1:
time: 113 us
  Pallas kernels  102 us (90%)
  local copies, waits for them, and re-layouts  8.92 us (8%)
  other arithmetic  1.35 us (1%)
    pallas_call x1, Pallas kernels, forward(): pl.pallas_call(functools.partial(block_kernel, nchip, ff_chunk, ff_slots)...  102 us
    unnamed x6, local copies, waits for them, and re-layouts  8.92 us

profile of v1, /device:TPU:113, one launch (start us, length us, event | category | flops | bytes accessed | tf_op | source)
XLA Modules:
  0.0 112.5 jit_solution(17905008872490562167)
XLA Ops:
  0.6 1.3 %fusion.bias_ref = f32[36,128]{1,0:T(8,128)} fusion(bf16[256]{0:T(256)(128)(2,1)} %param.39, bf16[2048]{0:T(1024)(128)(2,1)} %param.37, bf16[256]{0:T(256)(128)(2,1)} %param.28, bf16[2048]{0:T(1024)(128)(2,1)} %param.26), kind=kLoop, calls=%fused_computation.1 | loop fusion | flops 41472 | bytes 27648 | tf_op jit(solution)/shard_map/convert_element_type | solution.py:493
  2.0 101.6 %shard_map.253 = (bf16[64,2048]{1,0:T(8,128)(2,1)}, bf16[64,2048]{1,0:T(8,128)(2,1)}, bf16[128,128]{1,0:T(8,128)(2,1)}, bf16[128,128]{1,0:T(8,128)(2,1)}, bf16[1...) custom-call(bf16[64,2048]{1,0:T(8,128)(2,1)} %x_hbm.1, bf16[4096,128]{1,0:T(8,128)(2,1)} %bitcast.13, ...), custom_call_target="tpu_custom_call" | custom-call | tf_op jit(solution)/shard_map/pallas_call | solution.py:542
  103.6 1.7 %copy.34 = bf16[64,2048]{1,0:T(8,128)(2,1)} copy(bf16[64,2048]{1,0:T(8,128)(2,1)} %get-tuple-element.24) | data formatting | bytes 524288
  105.3 1.7 %copy.35 = bf16[64,2048]{1,0:T(8,128)(2,1)} copy(bf16[64,2048]{1,0:T(8,128)(2,1)} %get-tuple-element.25) | data formatting | bytes 524288
  106.9 1.4 %copy.36 = bf16[64,2,128]{2,1,0:T(2,128)(2,1)} copy(bf16[64,2,128]{2,1,0:T(2,128)(2,1)} %bitcast.20) | data formatting | bytes 65536
  108.3 1.4 %copy.37 = bf16[64,2,128]{2,1,0:T(2,128)(2,1)} copy(bf16[64,2,128]{2,1,0:T(2,128)(2,1)} %bitcast.19) | data formatting | bytes 65536
  109.7 1.4 %copy.38 = bf16[64,2,128]{2,1,0:T(2,128)(2,1)} copy(bf16[64,2,128]{2,1,0:T(2,128)(2,1)} %bitcast.18) | data formatting | bytes 65536
  111.1 1.4 %copy.39 = bf16[64,2,128]{2,1,0:T(2,128)(2,1)} copy(bf16[64,2,128]{2,1,0:T(2,128)(2,1)} %bitcast.17) | data formatting | bytes 65536

commit v2 on v1

--- a/solution.py
+++ b/solution.py
@@ -12,6 +12,7 @@
 ROPE_THETA = 500000.0
 NORM_EPS = 1e-5
 MESH = pl.DeviceIdType.MESH
+scope = jax.named_scope
 F32 = jnp.float32
 BF16 = jnp.bfloat16
 
@@ -36,11 +37,11 @@
 
 def block_kernel(nchip, ff_chunk, ff_slots,
                  x_hbm, kc1, vc1, wq1, wk1, wv1, wo1, w_gate, w_up, w_down, kc2, vc2, wq2, wk2, wv2, wo2,
-                 bias_ref, cos_hbm, sin_hbm,
+                 bq1, bk1, bq2, bk2, cos_hbm, sin_hbm,
                  g_out, y_out, k1_out, v1_out, k2_out, v2_out,
-                 xbuf, hbuf, ubuf, wqb, wkb, wvb, wob, kall, vtall, kstage, vstage, ksend, vsend, deint,
-                 qall, s_a, s_b, m_a, m_b, obuf, relay, final, ohalf, ysend, yrecv, macc, mrecv,
-                 w1s, w3s, w2s, ebuf, cosb, sinb, kvout, gout,
+                 xbuf, hbuf, ubuf, wkb, wvb, wob, kall, vtall, kstage, vstage, ksend, vsend, deint,
+                 qall, s_a, s_b, m_a, m_b, obuf, relay, final, ohalf, ysend, yrecv, mrecv,
+                 w1s, w3s, w2s, ebuf, cosb, sinb, bqb, bkb, kvout, gout,
                  dsem, rings, ssem, rsem):
     tok = x_hbm.shape[0]
     ctok = 2 * tok
@@ -65,6 +66,7 @@
     left = left_chip * 2 + core
     right = right_chip * 2 + core
 
+    macc = ysend
     dcount = [0]
 
     def local(src, dst):
@@ -98,10 +100,13 @@
     pos_rows = pl.ds(pl.multiple_of(chip * ctok, ctok), ctok)
     cp_cos = local(cos_hbm.at[pos_rows], cosb)
     cp_sin = local(sin_hbm.at[pos_rows], sinb)
+    cp_bq = [local(ref, bqb.at[la]) for la, ref in enumerate((bq1, bq2))]
+    cp_bk = [local(ref, bkb.at[la]) for la, ref in enumerate((bk1, bk2))]
     cp_ks = [local(kc[la], kstage) for la in range(2)]
     cp_vs = [local(vc[la], vstage) for la in range(2)]
     qcol = [pl.ds(pl.multiple_of(core * half_w + hp * rows, rows), rows) for hp in range(PAIRS)]
-    cp_wq = [[local(wq[la].at[:, qcol[hp]], wqb.at[hp]) for hp in range(PAIRS)] for la in range(2)]
+    wqb = [(w1s, w3s)[hp // 2].at[ff_slots - 1, :, pl.ds((hp % 2) * rows, rows)] for hp in range(PAIRS)]
+    cp_wq = [[local(wq[la].at[:, qcol[hp]], wqb[hp]) for hp in range(PAIRS)] for la in range(2)]
     cp_wk = [local(wk[la], wkb) for la in range(2)]
     cp_wv = [local(wv[la], wvb) for la in range(2)]
     cp_wo = [local(wo[la].at[pl.ds(pl.multiple_of(core * half_w, half_w), half_w)], wob) for la in range(2)]
@@ -115,24 +120,24 @@
     rc_v = [remote(vsend, vtall.at[la, :, pl.ds(keys_dev, keys_dev)], partner) for la in range(2)]
     rc_qr, rc_ql, rc_qf, rc_o = [], [], [], []
     for la in range(2):
-        own = [qall.at[la, SLOT["own%d" % hp]] for hp in range(PAIRS)]
-        rc_qr.append([remote(own[hp], qall.at[la, SLOT["left%d" % hp]], right) for hp in range(PAIRS)])
-        rc_ql.append([remote(own[hp], qall.at[la, SLOT["right%d" % hp]], left) for hp in range(PAIRS)])
+        own = [qall.at[SLOT["own%d" % hp]] for hp in range(PAIRS)]
+        rc_qr.append([remote(own[hp], qall.at[SLOT["left%d" % hp]], right) for hp in range(PAIRS)])
+        rc_ql.append([remote(own[hp], qall.at[SLOT["right%d" % hp]], left) for hp in range(PAIRS)])
         fwd = []
         for hp in range(PAIRS):
             side, dev = ("left", right) if hp % 2 == 0 else ("right", left)
-            fwd.append(remote(qall.at[la, SLOT["%s%d" % (side, hp)]], qall.at[la, SLOT["opp%d" % hp]], dev))
+            fwd.append(remote(qall.at[SLOT["%s%d" % (side, hp)]], qall.at[SLOT["opp%d" % hp]], dev))
         rc_qf.append(fwd)
         outs = {}
         for hp in range(PAIRS):
-            outs["left%d" % hp] = remote(obuf.at[SLOT["left%d" % hp]], final.at[la, 1, hp], left)
-            outs["right%d" % hp] = remote(obuf.at[SLOT["right%d" % hp]], final.at[la, 0, hp], right)
-            outs["opp%d" % hp] = remote(obuf.at[SLOT["opp%d" % hp]], relay.at[la, hp], right if hp % 2 == 0 else left)
+            outs["left%d" % hp] = remote(obuf.at[SLOT["left%d" % hp]], final.at[1, hp], left)
+            outs["right%d" % hp] = remote(obuf.at[SLOT["right%d" % hp]], final.at[0, hp], right)
+            outs["opp%d" % hp] = remote(obuf.at[SLOT["opp%d" % hp]], relay.at[hp], right if hp % 2 == 0 else left)
         rc_o.append(outs)
     rc_y1 = [remote(ysend.at[n], yrecv.at[n], partner) for n in range(ncol)]
     other_rows = pl.ds(pl.multiple_of((1 - core) * tok, tok), tok)
-    rc_y2 = [remote(ysend.at[n, other_rows], mrecv.at[n, pl.ds(ctok, tok)], partner) for n in range(ncol)]
-    rc_m = [remote(macc.at[n], mrecv.at[n, pl.ds(0, ctok)], partner) for n in range(ncol)]
+    rc_y2 = [remote(ysend.at[n, other_rows], yrecv.at[n, pl.ds(0, tok)], partner) for n in range(ncol)]
+    rc_m = [remote(macc.at[n], mrecv.at[n], partner) for n in range(ncol)]
 
     ff_half = w_gate.shape[1] // 2
     nfull = ff_half // ff_chunk
@@ -186,25 +191,23 @@
             cp_vs[1].start()
 
     def project(la, in_ref):
-        heads_all = wq1.shape[1] // hd
-        base = la * (heads_all + 2)
-
-        def bias_row(idx):
-            return bias_ref[pl.ds(idx, 1), :]
-
+        heads_half = half_w // hd
+        bq_v = bqb[la].astype(F32)
+        bq_v = jnp.where(core == 0, bq_v[:heads_half], bq_v[heads_half:])
+        bk_v = bkb[la].astype(F32)
         cos_v, sin_v = cosb[...], sinb[...]
         for hp in range(PAIRS):
             cp_wq[la][hp].wait()
-            acc = jnp.dot(in_ref[...], wqb[hp], preferred_element_type=F32)
+            acc = jnp.dot(in_ref[...], wqb[hp][...], preferred_element_type=F32)
             slot = SLOT["own%d" % hp]
             for j in range(2):
-                row = base + core * (heads_all // 2) + hp * 2 + j
-                qall[la, slot, pl.ds(j * ctok, ctok), :] = rope(acc[:, j * hd:(j + 1) * hd], bias_row(row), cos_v, sin_v)
+                row = hp * 2 + j
+                qall[slot, pl.ds(j * ctok, ctok), :] = rope(acc[:, j * hd:(j + 1) * hd], bq_v[row:row + 1], cos_v, sin_v)
             rc_qr[la][hp].start()
             rc_ql[la][hp].start()
         cp_wk[la].wait()
         acc = jnp.dot(in_ref[...], wkb[...], preferred_element_type=F32)
-        k_heads = [rope(acc[:, j * hd:(j + 1) * hd], bias_row(base + heads_all + j), cos_v, sin_v).astype(F32) for j in range(2)]
+        k_heads = [rope(acc[:, j * hd:(j + 1) * hd], bk_v[j:j + 1], cos_v, sin_v).astype(F32) for j in range(2)]
         cp_wv[la].wait()
         acc = jnp.dot(in_ref[...], wvb[...], preferred_element_type=F32)
         v_heads = [acc[:, j * hd:(j + 1) * hd].astype(BF16).astype(F32) for j in range(2)]
@@ -229,7 +232,7 @@
         return res
 
     def scores(la, unit, s_ref, m_ref):
-        s_val = lax.dot_general(kall[la], qall[la, unit], (((1,), (1,)), ((), ())), preferred_element_type=F32)
+        s_val = lax.dot_general(kall[la], qall[unit], (((1,), (1,)), ((), ())), preferred_element_type=F32)
         s_ref[pl.ds(0, keys_chip), :] = s_val[:keys_chip]
         peak = jnp.max(s_val[:keys_chip].reshape(keys_chip // 8, 8, rows), axis=0)
         key_i = lax.broadcasted_iota(jnp.int32, (ctok, rows), 0)
@@ -289,9 +292,11 @@
             merge_it = (name.startswith("right") and hp % 2 == 0) or (name.startswith("left") and hp % 2 == 1)
 
             def act(name=name, cp=cp, hp=hp, merge_it=merge_it):
+                if name.startswith("left" if hp % 2 == 0 else "right"):
+                    rc_qf[la][hp].wait_send()
                 if merge_it:
                     rc_o[la]["opp%d" % hp].wait_recv()
-                    put(obuf.at[SLOT[name]], *merged([get(obuf.at[SLOT[name]]), get(relay.at[la, hp])]))
+                    put(obuf.at[SLOT[name]], *merged([get(obuf.at[SLOT[name]]), get(relay.at[hp])]))
                 cp.start()
 
             acts[SLOT[name]] = [act]
@@ -300,7 +305,8 @@
     def attention(la):
         rc_k[la].wait_recv()
         rc_v[la].wait_recv()
-        scores(la, 0, s_a, m_a)
+        with scope("score0"):
+            scores(la, 0, s_a, m_a)
         pre, post = before(la), after(la)
 
         def run(acts, pair, parity):
@@ -308,8 +314,9 @@
                 if unit % 2 == parity:
                     @pl.when(pair == unit // 2)
                     def _(fns=fns):
-                        for fn in fns:
-                            fn()
+                        with scope("event"):
+                            for fn in fns:
+                                fn()
 
         def body(pair, _):
             run(pre, pair, 0)
@@ -324,9 +331,10 @@
 
     def finish_attention(la):
         for hp in range(PAIRS):
-            rc_o[la]["right%d" % hp].wait_recv()
-            rc_o[la]["left%d" % hp].wait_recv()
-            out_v, _, total = merged([get(obuf.at[SLOT["own%d" % hp]]), get(final.at[la, 0, hp]), get(final.at[la, 1, hp])])
+            with scope("owait"):
+                rc_o[la]["right%d" % hp].wait_recv()
+                rc_o[la]["left%d" % hp].wait_recv()
+            out_v, _, total = merged([get(obuf.at[SLOT["own%d" % hp]]), get(final.at[0, hp]), get(final.at[1, hp])])
             out_v = out_v / total
             for j in range(2):
                 ohalf[:, pl.ds((2 * hp + j) * hd, hd)] = out_v[:, j * ctok:(j + 1) * ctok].T.astype(BF16)
@@ -335,7 +343,7 @@
         for n in range(ncol):
             ysend[n] = jnp.dot(ohalf[...], wob[:, n * cw:(n + 1) * cw], preferred_element_type=F32)
             rc_y[n].start()
-        for cp in list(rc_qr[la]) + list(rc_ql[la]) + list(rc_qf[la]) + list(rc_o[la].values()):
+        for cp in list(rc_qr[la]) + list(rc_ql[la]) + list(rc_o[la].values()):
             cp.wait_send()
 
     def normed(wide):
@@ -351,33 +359,43 @@
     cp_x.start()
     cp_cos.start()
     cp_sin.start()
+    for cp in cp_bq + cp_bk:
+        cp.start()
     cp_ks[0].start()
     cp_vs[0].start()
     for hp in range(PAIRS):
         cp_wq[0][hp].start()
     cp_wk[0].start()
     cp_wv[0].start()
-    pl.semaphore_wait(barrier, 3)
+    with scope("entry"):
+        pl.semaphore_wait(barrier, 3)
     rc_x.start()
-    prep_cache(0)
+    with scope("prep0"):
+        prep_cache(0)
     cp_cos.wait()
     cp_sin.wait()
+    for cp in cp_bq + cp_bk:
+        cp.wait()
     cp_x.wait()
-    rc_x.wait_recv()
-    project(0, xbuf)
-    for hp in range(PAIRS):
-        cp_wq[1][hp].start()
+    with scope("xwait"):
+        rc_x.wait_recv()
+    with scope("proj0"):
+        project(0, xbuf)
+    cp_wo[0].start()
     cp_wk[1].start()
     cp_wv[1].start()
-    cp_wo[0].start()
     for slot in range(ff_slots):
         for cp in ff_copies(slot, slot, ff_chunk):
             cp.start()
-    attention(0)
-    prep_cache(1)
-    finish_attention(0)
-    for n in range(ncol):
-        rc_y1[n].wait()
+    with scope("attn0"):
+        attention(0)
+    with scope("prep1"):
+        prep_cache(1)
+    with scope("fin0"):
+        finish_attention(0)
+    with scope("ywait"):
+        for n in range(ncol):
+            rc_y1[n].wait()
 
     def first_norm(rs):
         parts = [(ysend[n, rs, :] + yrecv[n, rs, :]).astype(BF16).astype(F32) for n in range(ncol)]
@@ -385,17 +403,19 @@
         hbuf[rs, :] = res
         ubuf[rs, :] = normed(res.astype(F32))
 
-    row_loop(ctok, first_norm)
-    cp_wo[1].start()
+    with scope("norm1"):
+        row_loop(ctok, first_norm)
 
     def gate_up(slot, size):
         gate = jnp.dot(ubuf[...], w1s[slot, :, pl.ds(0, size)], preferred_element_type=F32).astype(BF16).astype(F32)
         up = jnp.dot(ubuf[...], w3s[slot, :, pl.ds(0, size)], preferred_element_type=F32).astype(BF16).astype(F32)
         return (jax.nn.silu(gate) * up).astype(BF16)
 
-    def down(slot, size):
+    def down(slot, size, send=False):
         for n in range(ncol):
             macc[n] += jnp.dot(ebuf[:, pl.ds(0, size)], w2s[slot, pl.ds(0, size), pl.ds(n * cw, cw)], preferred_element_type=F32)
+            if send:
+                rc_m[n].start()
 
     def refill(chunk, which):
         for size, cond in ((ff_chunk, chunk < nfull), (tail, chunk == nfull)):
@@ -426,7 +446,11 @@
         refill(k - 1 + ff_slots, (2,))
         return 0
 
-    lax.fori_loop(1, nfull, mlp_body, 0)
+    with scope("mlp"):
+        lax.fori_loop(1, nfull, mlp_body, 0)
+    for hp in range(PAIRS):
+        cp_wq[1][hp].start()
+    cp_wo[1].start()
     last_slot = (nfull - 1) % ff_slots
     ff_copies(nfull - 1, last_slot, ff_chunk)[2].wait()
     if tail:
@@ -438,13 +462,12 @@
         down(last_slot, ff_chunk)
         ebuf[:, pl.ds(0, tail)] = hidden
         cps[2].wait()
-        down(slot, tail)
+        down(slot, tail, send=True)
     else:
-        down(last_slot, ff_chunk)
-    for n in range(ncol):
-        rc_m[n].start()
-    for n in range(ncol):
-        rc_m[n].wait()
+        down(last_slot, ff_chunk, send=True)
+    with scope("mwait"):
+        for n in range(ncol):
+            rc_m[n].wait()
 
     def second_norm(rs):
         acc = jnp.concatenate([macc[n, rs, :] + mrecv[n, rs, :] for n in range(ncol)], axis=1)
@@ -452,16 +475,20 @@
         hbuf[rs, :] = res
         ubuf[rs, :] = normed(res.astype(F32))
 
-    row_loop(ctok, second_norm)
+    with scope("norm2"):
+        row_loop(ctok, second_norm)
     gout[0] = hbuf[my_rows, :]
     cp_g.start()
 
-    project(1, ubuf)
-    attention(1)
-    finish_attention(1)
+    with scope("proj1"):
+        project(1, ubuf)
+    with scope("attn1"):
+        attention(1)
+    with scope("fin1"):
+        finish_attention(1)
     for n in range(ncol):
         rc_y2[n].wait()
-        gout[1, :, pl.ds(n * cw, cw)] = (ysend[n, my_rows, :] + mrecv[n, pl.ds(ctok, tok), :]).astype(BF16)
+        gout[1, :, pl.ds(n * cw, cw)] = (ysend[n, my_rows, :] + yrecv[n, pl.ds(0, tok), :]).astype(BF16)
     cp_y.start()
     rc_x.wait_send()
     rc_k[1].wait_send()
@@ -470,10 +497,16 @@
         cp.wait()
 
 
+def copy_out(*refs):
+    half = len(refs) // 2
+    for src, dst in zip(refs[:half], refs[half:]):
+        dst[...] = src[...]
+
+
 def solution(mesh):
     axis_size = mesh.shape["cp"]
     nchip = axis_size // 2
-    ff_chunk, ff_slots = 512, 3
+    ff_chunk, ff_slots = 512, 5
     rows_spec = P(("dp", "cp"), None)
     cache_spec = P(("dp", "cp"), None, None)
     mat_spec = P(None, None)
@@ -490,17 +523,14 @@
         rows = 2 * ctok
         keys_tot = 2 * cache_dev + ctok
         cos_t, sin_t = rope_tables(axis_size * cache_dev, axis_size * tok, hd)
-        bias = jnp.concatenate([b_q1, b_k1, b_q2, b_k2]).astype(F32).reshape(-1, hd)
         flat = lambda arr: arr.reshape(-1, hd)
         half_w = width // 2
         ncol = 4
         hbm = pl.BlockSpec(memory_space=pl.ANY)
-        vmem = pl.BlockSpec(memory_space=pltpu.VMEM)
         scratch = [
             pltpu.VMEM((ctok, width), BF16),
             pltpu.VMEM((ctok, width), BF16),
             pltpu.VMEM((ctok, width), BF16),
-            pltpu.VMEM((PAIRS, width, rows), BF16),
             pltpu.VMEM(w_k1.shape, BF16),
             pltpu.VMEM(w_v1.shape, BF16),
             pltpu.VMEM((half_w, width), BF16),
@@ -511,28 +541,29 @@
             pltpu.VMEM((cache_dev, hd), BF16),
             pltpu.VMEM((hd, cache_dev), BF16),
             pltpu.VMEM((2 * hd, hd), F32),
-            pltpu.VMEM((2, UNITS, rows, hd), BF16),
+            pltpu.VMEM((UNITS, rows, hd), BF16),
             pltpu.VMEM((keys_tot, rows), F32),
             pltpu.VMEM((keys_tot, rows), F32),
             pltpu.VMEM((8, rows), F32),
             pltpu.VMEM((8, rows), F32),
             pltpu.VMEM((UNITS, hd + 8, rows), F32),
+            pltpu.VMEM((PAIRS, hd + 8, rows), F32),
             pltpu.VMEM((2, PAIRS, hd + 8, rows), F32),
-            pltpu.VMEM((2, 2, PAIRS, hd + 8, rows), F32),
             pltpu.VMEM((ctok, half_w), BF16),
             pltpu.VMEM((ncol, ctok, width // ncol), F32),
             pltpu.VMEM((ncol, ctok, width // ncol), F32),
             pltpu.VMEM((ncol, ctok, width // ncol), F32),
-            pltpu.VMEM((ncol, ctok + tok, width // ncol), F32),
             pltpu.VMEM((ff_slots, width, ff_chunk), BF16),
             pltpu.VMEM((ff_slots, width, ff_chunk), BF16),
             pltpu.VMEM((ff_slots, ff_chunk, width), BF16),
             pltpu.VMEM((ctok, ff_chunk), BF16),
             pltpu.VMEM((ctok, hd), F32),
             pltpu.VMEM((ctok, hd), F32),
+            pltpu.VMEM((2, width // hd, hd), BF16),
+            pltpu.VMEM((2, kv_heads, hd), BF16),
             pltpu.VMEM((2, 2, 2 * tok, hd), BF16),
             pltpu.VMEM((2, tok, width), BF16),
-            pltpu.SemaphoreType.DMA((29,)),
+            pltpu.SemaphoreType.DMA((33,)),
             pltpu.SemaphoreType.DMA((3, ff_slots)),
             pltpu.SemaphoreType.DMA((65,)),
             pltpu.SemaphoreType.DMA((65,)),
@@ -542,12 +573,14 @@
         outs = pl.pallas_call(
             functools.partial(block_kernel, nchip, ff_chunk, ff_slots),
             out_shape=(act, act, app, app, app, app),
-            in_specs=[hbm] * 16 + [vmem, hbm, hbm],
+            in_specs=[hbm] * 22,
             out_specs=(hbm,) * 6,
             scratch_shapes=scratch,
             compiler_params=pltpu.CompilerParams(collective_id=0, has_side_effects=True, vmem_limit_bytes=67043328),
         )(x_in, flat(cache_k1), flat(cache_v1), w_q1, w_k1, w_v1, w_o1, w_gate, w_up, w_down,
-          flat(cache_k2), flat(cache_v2), w_q2, w_k2, w_v2, w_o2, bias, jnp.asarray(cos_t), jnp.asarray(sin_t))
+          flat(cache_k2), flat(cache_v2), w_q2, w_k2, w_v2, w_o2,
+          flat(b_q1), flat(b_k1), flat(b_q2), flat(b_k2), jnp.asarray(cos_t), jnp.asarray(sin_t))
+        outs = pl.pallas_call(copy_out, out_shape=[jax.ShapeDtypeStruct(arr.shape, arr.dtype) for arr in outs])(*outs)
         hidden, y_two = outs[:2]
         appends = [arr.reshape(tok, kv_heads, hd) for arr in outs[2:]]
         return (hidden, y_two, *appends)

time: 113 us -> 99.2 us (0.88)
  local copies, waits for them, and re-layouts: 8.92 us -> 0 us
  Pallas kernels: 102 us -> 98.5 us
  other arithmetic: 1.35 us -> 0 us
    unnamed x6 -> x0, local copies, waits for them, and re-layouts: 8.92 us -> none
    pallas_call x1, Pallas kernels: 102 us -> 96.6 us  [forward(): pl.pallas_call(functools.partial(block_kernel, nchip, ff_chunk, ff_slots)...]
    pallas_call x0 -> x1, Pallas kernels: none -> 1.9 us  [forward(): pl.pallas_call(copy_out, out_shape=[jax.ShapeDtypeStruct(arr.shape, arr.d...]
    convert_element_type x1 -> x0, other arithmetic: 1.35 us -> none  [forward(): bias = jnp.concatenate([b_q1, b_k1, b_q2, b_k2]).astype(F32).reshape(-1, hd)]
where the time goes in v2:
time: 99.2 us; the launch traced here: 99.1 us
  Pallas kernels  98.5 us (99%)
    pallas_call x1, Pallas kernels, forward(): pl.pallas_call(functools.partial(block_kernel, nchip, ff_chunk, ff_slots)...  96.6 us

profile of v2, /device:TPU:113, one launch (start us, length us, event | category | flops | bytes accessed | tf_op | source)
XLA Modules:
  0.0 99.1 jit_solution(1322663295476190054)
XLA Ops:
  0.6 96.6 %shard_map.253 = (bf16[64,2048]{1,0:T(8,128)(2,1)}, bf16[64,2048]{1,0:T(8,128)(2,1)}, bf16[128,128]{1,0:T(8,128)(2,1)}, bf16[128,128]{1,0:T(8,128)(2,1)}, bf16[1...) custom-call(bf16[64,2048]{1,0:T(8,128)(2,1)} %x_hbm.1, bf16[4096,128]{1,0:T(8,128)(2,1)} %bitcast.12, ...), custom_call_target="tpu_custom_call" | custom-call | tf_op jit(solution)/shard_map/pallas_call | solution.py:573
  97.2 1.9 %shard_map.254 = (bf16[64,2048]{1,0:T(8,128)(2,1)}, bf16[64,2048]{1,0:T(8,128)(2,1)}, bf16[128,128]{1,0:T(8,128)(2,1)}, bf16[128,128]{1,0:T(8,128)(2,1)}, bf16[1...) custom-call(bf16[64,2048]{1,0:T(8,128)(2,1)} %get-tuple-element.18.refs_0_, bf16[64,2048]{1,0:T(8,128)(2,1)} %get-tuple-element.19.refs_1_, ...), custom_call_target="tpu_custom_call" | custom-call | tf_op jit(solution)/shard_map/pallas_call | solution.py:583

commit v3 on v2

--- a/solution.py
+++ b/solution.py
@@ -16,12 +16,13 @@
 F32 = jnp.float32
 BF16 = jnp.bfloat16
 
-ORDER = ("own0", "own1", "own2", "left0", "right1", "opp0", "opp1", "left2", "right3", "opp2", "opp3",
-         "right0", "left1", "right2", "left3", "own3")
+ORDER = ("own0", "left0", "right1", "left2", "opp0", "opp1", "right3", "opp2", "opp3",
+         "right0", "left1", "own1", "right2", "left3", "own2", "own3")
+FORWARD_BEFORE = (0, 1, 2, 3)
 SLOT = {name: idx for idx, name in enumerate(ORDER)}
 UNITS = len(ORDER)
 PAIRS = 4
-NORM_ROWS = 16
+NORM_ROWS = 32
 
 
 def rope_tables(first_pos, count, head_dim):
@@ -35,12 +36,12 @@
     return np.concatenate([cos_t, cos_t], axis=1), np.concatenate([-sin_t, sin_t], axis=1)
 
 
-def block_kernel(nchip, ff_chunk, ff_slots,
+def block_kernel(nchip, ff_first, ff_chunk, ff_slots,
                  x_hbm, kc1, vc1, wq1, wk1, wv1, wo1, w_gate, w_up, w_down, kc2, vc2, wq2, wk2, wv2, wo2,
                  bq1, bk1, bq2, bk2, cos_hbm, sin_hbm,
                  g_out, y_out, k1_out, v1_out, k2_out, v2_out,
-                 xbuf, hbuf, ubuf, wkb, wvb, wob, kall, vtall, kstage, vstage, ksend, vsend, deint,
-                 qall, s_a, s_b, m_a, m_b, obuf, relay, final, ohalf, ysend, yrecv, mrecv,
+                 xbuf, hbuf, ubuf, wkvb, wob, kall, vtall, kstage, vstage, ksend, vsend, deint,
+                 qall, m_a, m_b, obuf, relay, final, ohalf, ysend, yrecv, mrecv,
                  w1s, w3s, w2s, ebuf, cosb, sinb, bqb, bkb, kvout, gout,
                  dsem, rings, ssem, rsem):
     tok = x_hbm.shape[0]
@@ -104,11 +105,11 @@
     cp_bk = [local(ref, bkb.at[la]) for la, ref in enumerate((bk1, bk2))]
     cp_ks = [local(kc[la], kstage) for la in range(2)]
     cp_vs = [local(vc[la], vstage) for la in range(2)]
-    qcol = [pl.ds(pl.multiple_of(core * half_w + hp * rows, rows), rows) for hp in range(PAIRS)]
-    wqb = [(w1s, w3s)[hp // 2].at[ff_slots - 1, :, pl.ds((hp % 2) * rows, rows)] for hp in range(PAIRS)]
-    cp_wq = [[local(wq[la].at[:, qcol[hp]], wqb[hp]) for hp in range(PAIRS)] for la in range(2)]
-    cp_wk = [local(wk[la], wkb) for la in range(2)]
-    cp_wv = [local(wv[la], wvb) for la in range(2)]
+    qcol = [pl.ds(pl.multiple_of(core * half_w + half * 2 * rows, rows), 2 * rows) for half in range(2)]
+    wqb = [ref.at[ff_slots - 1, :, pl.ds(0, 2 * rows)] for ref in (w1s, w3s)]
+    cp_wq = [[local(wq[la].at[:, qcol[half]], wqb[half]) for half in range(2)] for la in range(2)]
+    cp_wk = [local(wk[la], wkvb.at[:, pl.ds(0, 2 * hd)]) for la in range(2)]
+    cp_wv = [local(wv[la], wkvb.at[:, pl.ds(2 * hd, 2 * hd)]) for la in range(2)]
     cp_wo = [local(wo[la].at[pl.ds(pl.multiple_of(core * half_w, half_w), half_w)], wob) for la in range(2)]
     cp_kout = [local(kvout.at[la, 0], k_out[la]) for la in range(2)]
     cp_vout = [local(kvout.at[la, 1], v_out[la]) for la in range(2)]
@@ -140,11 +141,11 @@
     rc_m = [remote(macc.at[n], mrecv.at[n], partner) for n in range(ncol)]
 
     ff_half = w_gate.shape[1] // 2
-    nfull = ff_half // ff_chunk
-    tail = ff_half - nfull * ff_chunk
+    nfull = (ff_half - ff_first) // ff_chunk
+    tail = ff_half - ff_first - nfull * ff_chunk
 
     def ff_copies(chunk, slot, size):
-        cols = pl.ds(pl.multiple_of(core * ff_half + chunk * ff_chunk, 128), size)
+        cols = pl.ds(pl.multiple_of(core * ff_half + ff_first + chunk * ff_chunk, 128), size)
         return (pltpu.make_async_copy(w_gate.at[:, cols], w1s.at[slot, :, pl.ds(0, size)], rings.at[0, slot]),
                 pltpu.make_async_copy(w_up.at[:, cols], w3s.at[slot, :, pl.ds(0, size)], rings.at[1, slot]),
                 pltpu.make_async_copy(w_down.at[cols], w2s.at[slot, pl.ds(0, size)], rings.at[2, slot]))
@@ -157,34 +158,34 @@
         if la == 1:
             rc_k[0].wait_send()
             rc_v[0].wait_send()
-        step_rows = 2 * hd
+        blk = deint.shape[0] // 2
 
         def split(ref, i):
-            deint[...] = ref[pl.ds(pl.multiple_of(i * step_rows, step_rows), step_rows), :].astype(F32)
-            head0 = deint[pl.ds(0, hd, stride=2), :]
-            head1 = deint[pl.ds(1, hd, stride=2), :]
+            deint[...] = ref[pl.ds(pl.multiple_of(i * 2 * blk, 2 * blk), 2 * blk), :].astype(F32)
+            head0 = deint[pl.ds(0, blk, stride=2), :]
+            head1 = deint[pl.ds(1, blk, stride=2), :]
             is0 = core == 0
             return jnp.where(is0, head0, head1), jnp.where(is0, head1, head0)
 
         def kbody(i, _):
             mine, other = split(kstage, i)
-            at = pl.ds(pl.multiple_of(i * hd, hd), hd)
+            at = pl.ds(pl.multiple_of(i * blk, blk), blk)
             kall[la, at, :] = mine.astype(BF16)
             ksend[at, :] = other.astype(BF16)
             return 0
 
         def vbody(i, _):
             mine, other = split(vstage, i)
-            at = pl.ds(pl.multiple_of(i * hd, hd), hd)
+            at = pl.ds(pl.multiple_of(i * blk, blk), blk)
             vtall[la, :, at] = mine.T.astype(BF16)
             vsend[:, at] = other.T.astype(BF16)
             return 0
 
         cp_ks[la].wait()
-        lax.fori_loop(0, keys_dev // hd, kbody, 0)
+        lax.fori_loop(0, keys_dev // blk, kbody, 0)
         rc_k[la].start()
         cp_vs[la].wait()
-        lax.fori_loop(0, keys_dev // hd, vbody, 0)
+        lax.fori_loop(0, keys_dev // blk, vbody, 0)
         rc_v[la].start()
         if la == 0:
             cp_ks[1].start()
@@ -196,20 +197,22 @@
         bq_v = jnp.where(core == 0, bq_v[:heads_half], bq_v[heads_half:])
         bk_v = bkb[la].astype(F32)
         cos_v, sin_v = cosb[...], sinb[...]
-        for hp in range(PAIRS):
-            cp_wq[la][hp].wait()
-            acc = jnp.dot(in_ref[...], wqb[hp][...], preferred_element_type=F32)
-            slot = SLOT["own%d" % hp]
-            for j in range(2):
-                row = hp * 2 + j
-                qall[slot, pl.ds(j * ctok, ctok), :] = rope(acc[:, j * hd:(j + 1) * hd], bq_v[row:row + 1], cos_v, sin_v)
-            rc_qr[la][hp].start()
-            rc_ql[la][hp].start()
+        for half in range(2):
+            cp_wq[la][half].wait()
+            acc = jnp.dot(in_ref[...], wqb[half][...], preferred_element_type=F32)
+            for hp in (2 * half, 2 * half + 1):
+                slot = SLOT["own%d" % hp]
+                for j in range(2):
+                    row = hp * 2 + j
+                    at = (row - 4 * half) * hd
+                    qall[slot, pl.ds(j * ctok, ctok), :] = rope(acc[:, at:at + hd], bq_v[row:row + 1], cos_v, sin_v)
+                rc_qr[la][hp].start()
+                rc_ql[la][hp].start()
         cp_wk[la].wait()
-        acc = jnp.dot(in_ref[...], wkb[...], preferred_element_type=F32)
+        cp_wv[la].wait()
+        acc = jnp.dot(in_ref[...], wkvb[...], preferred_element_type=F32)
         k_heads = [rope(acc[:, j * hd:(j + 1) * hd], bk_v[j:j + 1], cos_v, sin_v).astype(F32) for j in range(2)]
-        cp_wv[la].wait()
-        acc = jnp.dot(in_ref[...], wvb[...], preferred_element_type=F32)
+        acc = acc[:, 2 * hd:]
         v_heads = [acc[:, j * hd:(j + 1) * hd].astype(BF16).astype(F32) for j in range(2)]
         is0 = core == 0
         kall[la, pl.ds(keys_chip, ctok), :] = jnp.where(is0, k_heads[0], k_heads[1]).astype(BF16)
@@ -241,14 +244,16 @@
         s_ref[pl.ds(keys_chip, ctok), :] = masked
         m_ref[...] = jnp.maximum(peak, jnp.max(masked.reshape(ctok // 8, 8, rows), axis=0))
 
-    row8 = lax.broadcasted_iota(jnp.int32, (8, rows), 0)
-
-    def put(dst, out_v, peak, total):
-        dst[pl.ds(0, hd), :] = out_v
-        dst[pl.ds(hd, 8), :] = jnp.where(row8 == 0, peak, total)
+    row8 = lax.broadcasted_iota(jnp.int32, (8, ctok), 0)
+
+    def put(dst, heads):
+        for h, (out_v, _, _) in enumerate(heads):
+            dst[pl.ds(h * hd, hd), :] = out_v
+        (_, peak0, total0), (_, peak1, total1) = heads
+        dst[pl.ds(2 * hd, 8), :] = jnp.where(row8 == 0, peak0, jnp.where(row8 == 1, peak1, jnp.where(row8 == 2, total0, total1)))
 
     def get(src):
-        return src[pl.ds(0, hd), :], src[pl.ds(hd, 1), :], src[pl.ds(hd + 1, 1), :]
+        return [(src[pl.ds(h * hd, hd), :], src[pl.ds(2 * hd + h, 1), :], src[pl.ds(2 * hd + 2 + h, 1), :]) for h in range(2)]
 
     def merged(parts):
         peak = functools.reduce(jnp.maximum, [part[1] for part in parts])
@@ -256,6 +261,9 @@
         out_v = functools.reduce(jnp.add, [part[0] * sc for part, sc in zip(parts, scales)])
         total = functools.reduce(jnp.add, [part[2] * sc for part, sc in zip(parts, scales)])
         return out_v, peak, total
+
+    def merged_heads(refs):
+        return [merged(parts) for parts in zip(*[get(ref) for ref in refs])]
 
     def attend_unit(la, unit, nxt, s_cur, m_cur, s_nxt, m_nxt):
         peak = jnp.max(m_cur[...], axis=0, keepdims=True)
@@ -264,7 +272,7 @@
         total = jnp.sum(jnp.sum(prob, axis=0), axis=0, keepdims=True)
         out_v = jnp.dot(vtall[la], prob.reshape(keys_tot, rows).astype(BF16), preferred_element_type=F32)
         scores(la, nxt, s_nxt, m_nxt)
-        put(obuf.at[unit], out_v, peak, total)
+        put(obuf.at[unit], [tuple(val[:, h * ctok:(h + 1) * ctok] for val in (out_v, peak, total)) for h in range(2)])
 
     def before(la):
         acts = {}
@@ -276,10 +284,10 @@
             lw, rw = rc_qr[la][hp].wait_recv, rc_ql[la][hp].wait_recv
             fwd = rc_qf[la][hp]
             if hp % 2 == 0:
-                acts.setdefault(2 if hp == 0 else 4, []).extend([lw, fwd.start])
+                acts.setdefault(FORWARD_BEFORE[hp], []).extend([lw, fwd.start])
                 add("right%d" % hp, rw)
             else:
-                acts.setdefault(3 if hp == 1 else 5, []).extend([rw, fwd.start])
+                acts.setdefault(FORWARD_BEFORE[hp], []).extend([rw, fwd.start])
                 add("left%d" % hp, lw)
         for hp in range(PAIRS):
             add("opp%d" % hp, rc_qf[la][hp].wait_recv)
@@ -296,13 +304,16 @@
                     rc_qf[la][hp].wait_send()
                 if merge_it:
                     rc_o[la]["opp%d" % hp].wait_recv()
-                    put(obuf.at[SLOT[name]], *merged([get(obuf.at[SLOT[name]]), get(relay.at[hp])]))
+                    put(obuf.at[SLOT[name]], merged_heads([obuf.at[SLOT[name]], relay.at[hp]]))
                 cp.start()
 
             acts[SLOT[name]] = [act]
         return acts
 
     def attention(la):
+        pl.run_scoped(functools.partial(attend_all, la), pltpu.VMEM((keys_tot, rows), F32), pltpu.VMEM((keys_tot, rows), F32))
+
+    def attend_all(la, s_a, s_b):
         rc_k[la].wait_recv()
         rc_v[la].wait_recv()
         with scope("score0"):
@@ -334,10 +345,9 @@
             with scope("owait"):
                 rc_o[la]["right%d" % hp].wait_recv()
                 rc_o[la]["left%d" % hp].wait_recv()
-            out_v, _, total = merged([get(obuf.at[SLOT["own%d" % hp]]), get(final.at[0, hp]), get(final.at[1, hp])])
-            out_v = out_v / total
-            for j in range(2):
-                ohalf[:, pl.ds((2 * hp + j) * hd, hd)] = out_v[:, j * ctok:(j + 1) * ctok].T.astype(BF16)
+            heads = merged_heads([obuf.at[SLOT["own%d" % hp]], final.at[0, hp], final.at[1, hp]])
+            for h, (out_v, _, total) in enumerate(heads):
+                ohalf[:, pl.ds((2 * hp + h) * hd, hd)] = (out_v / total).T.astype(BF16)
         cp_wo[la].wait()
         rc_y = (rc_y1, rc_y2)[la]
         for n in range(ncol):
@@ -363,8 +373,8 @@
         cp.start()
     cp_ks[0].start()
     cp_vs[0].start()
-    for hp in range(PAIRS):
-        cp_wq[0][hp].start()
+    for half in range(2):
+        cp_wq[0][half].start()
     cp_wk[0].start()
     cp_wv[0].start()
     with scope("entry"):
@@ -389,97 +399,124 @@
             cp.start()
     with scope("attn0"):
         attention(0)
-    with scope("prep1"):
-        prep_cache(1)
-    with scope("fin0"):
-        finish_attention(0)
-    with scope("ywait"):
-        for n in range(ncol):
-            rc_y1[n].wait()
-
-    def first_norm(rs):
-        parts = [(ysend[n, rs, :] + yrecv[n, rs, :]).astype(BF16).astype(F32) for n in range(ncol)]
-        res = (xbuf[rs, :].astype(F32) + jnp.concatenate(parts, axis=1)).astype(BF16)
-        hbuf[rs, :] = res
-        ubuf[rs, :] = normed(res.astype(F32))
-
-    with scope("norm1"):
-        row_loop(ctok, first_norm)
-
-    def gate_up(slot, size):
-        gate = jnp.dot(ubuf[...], w1s[slot, :, pl.ds(0, size)], preferred_element_type=F32).astype(BF16).astype(F32)
-        up = jnp.dot(ubuf[...], w3s[slot, :, pl.ds(0, size)], preferred_element_type=F32).astype(BF16).astype(F32)
-        return (jax.nn.silu(gate) * up).astype(BF16)
-
-    def down(slot, size, send=False):
-        for n in range(ncol):
-            macc[n] += jnp.dot(ebuf[:, pl.ds(0, size)], w2s[slot, pl.ds(0, size), pl.ds(n * cw, cw)], preferred_element_type=F32)
-            if send:
-                rc_m[n].start()
-
-    def refill(chunk, which):
-        for size, cond in ((ff_chunk, chunk < nfull), (tail, chunk == nfull)):
-            if size:
-                @pl.when(cond)
-                def _(size=size):
-                    cps = ff_copies(chunk, lax.rem(chunk, ff_slots), size)
-                    for w in which:
-                        cps[w].start()
-
-    macc[...] = jnp.zeros(macc.shape, F32)
-    first = ff_copies(0, 0, ff_chunk)
-    first[0].wait()
-    first[1].wait()
-    ebuf[...] = gate_up(0, ff_chunk)
-    refill(jnp.int32(ff_slots), (0, 1))
-
-    def mlp_body(k, _):
-        slot, prev = lax.rem(k, ff_slots), lax.rem(k - 1, ff_slots)
-        cps = ff_copies(k, slot, ff_chunk)
-        cps[0].wait()
-        cps[1].wait()
-        ff_copies(k - 1, prev, ff_chunk)[2].wait()
-        hidden = gate_up(slot, ff_chunk)
-        down(prev, ff_chunk)
-        ebuf[...] = hidden
-        refill(k + ff_slots, (0, 1))
-        refill(k - 1 + ff_slots, (2,))
-        return 0
-
-    with scope("mlp"):
-        lax.fori_loop(1, nfull, mlp_body, 0)
-    for hp in range(PAIRS):
-        cp_wq[1][hp].start()
-    cp_wo[1].start()
-    last_slot = (nfull - 1) % ff_slots
-    ff_copies(nfull - 1, last_slot, ff_chunk)[2].wait()
-    if tail:
-        slot = nfull % ff_slots
-        cps = ff_copies(nfull, slot, tail)
-        cps[0].wait()
-        cps[1].wait()
-        hidden = gate_up(slot, tail)
-        down(last_slot, ff_chunk)
-        ebuf[:, pl.ds(0, tail)] = hidden
-        cps[2].wait()
-        down(slot, tail, send=True)
-    else:
-        down(last_slot, ff_chunk, send=True)
-    with scope("mwait"):
-        for n in range(ncol):
-            rc_m[n].wait()
-
-    def second_norm(rs):
-        acc = jnp.concatenate([macc[n, rs, :] + mrecv[n, rs, :] for n in range(ncol)], axis=1)
-        res = (hbuf[rs, :].astype(F32) + acc).astype(BF16)
-        hbuf[rs, :] = res
-        ubuf[rs, :] = normed(res.astype(F32))
-
-    with scope("norm2"):
-        row_loop(ctok, second_norm)
-    gout[0] = hbuf[my_rows, :]
-    cp_g.start()
-
+    def middle(w1f, w3f, w2f):
+        cols = pl.ds(pl.multiple_of(core * ff_half, 128), ff_first)
+        cp_first = [local(w_gate.at[:, cols], w1f), local(w_up.at[:, cols], w3f), local(w_down.at[cols], w2f)]
+        for cp in cp_first:
+            cp.start()
+        with scope("prep1"):
+            prep_cache(1)
+        with scope("fin0"):
+            finish_attention(0)
+        with scope("ywait"):
+            for n in range(ncol):
+                rc_y1[n].wait()
+
+        def first_norm(rs):
+            parts = [(ysend[n, rs, :] + yrecv[n, rs, :]).astype(BF16).astype(F32) for n in range(ncol)]
+            res = (xbuf[rs, :].astype(F32) + jnp.concatenate(parts, axis=1)).astype(BF16)
+            hbuf[rs, :] = res
+            ubuf[rs, :] = normed(res.astype(F32))
+
+        with scope("norm1"):
+            row_loop(ctok, first_norm)
+
+        def gate_up(w1, w3):
+            gate = jnp.dot(ubuf[...], w1[...], preferred_element_type=F32).astype(BF16).astype(F32)
+            up = jnp.dot(ubuf[...], w3[...], preferred_element_type=F32).astype(BF16).astype(F32)
+            return (jax.nn.silu(gate) * up).astype(BF16)
+
+        def down(w2, size, init=False, send=False):
+            for n in range(ncol):
+                part = jnp.dot(ebuf[:, pl.ds(0, size)], w2[:, pl.ds(n * cw, cw)], preferred_element_type=F32)
+                if init:
+                    macc[n] = part
+                else:
+                    macc[n] += part
+                if send:
+                    rc_m[n].start()
+
+        def ring_up(slot, size):
+            return gate_up(w1s.at[slot, :, pl.ds(0, size)], w3s.at[slot, :, pl.ds(0, size)])
+
+        def ring_down(slot, size, send=False):
+            down(w2s.at[slot, pl.ds(0, size)], size, send=send)
+
+        def refill(chunk, which):
+            for size, cond in ((ff_chunk, chunk < nfull), (tail, chunk == nfull)):
+                if size:
+                    @pl.when(cond)
+                    def _(size=size):
+                        cps = ff_copies(chunk, lax.rem(chunk, ff_slots), size)
+                        for w in which:
+                            cps[w].start()
+
+        with scope("mlp_a"):
+            cp_first[0].wait()
+            cp_first[1].wait()
+            ebuf[:, pl.ds(0, ff_first)] = gate_up(w1f, w3f)
+            ready = ff_copies(0, 0, ff_chunk)
+            ready[0].wait()
+            ready[1].wait()
+            cp_first[2].wait()
+            hidden = ring_up(0, ff_chunk)
+            down(w2f, ff_first, init=True)
+            ebuf[:, pl.ds(0, ff_chunk)] = hidden
+            refill(jnp.int32(ff_slots), (0, 1))
+
+        def mlp_body(k, _):
+            slot, prev = lax.rem(k, ff_slots), lax.rem(k - 1, ff_slots)
+            cps = ff_copies(k, slot, ff_chunk)
+            with scope("stream"):
+                cps[0].wait()
+                cps[1].wait()
+                ff_copies(k - 1, prev, ff_chunk)[2].wait()
+            hidden = ring_up(slot, ff_chunk)
+            ring_down(prev, ff_chunk)
+            ebuf[:, pl.ds(0, ff_chunk)] = hidden
+            refill(k + ff_slots, (0, 1))
+            refill(k - 1 + ff_slots, (2,))
+            return 0
+
+        with scope("mlp"):
+            lax.fori_loop(1, nfull, mlp_body, 0)
+        last_slot = (nfull - 1) % ff_slots
+        with scope("mlp_z"):
+            ff_copies(nfull - 1, last_slot, ff_chunk)[2].wait()
+            if tail:
+                slot = nfull % ff_slots
+                cps = ff_copies(nfull, slot, tail)
+                cps[0].wait()
+                cps[1].wait()
+                hidden = ring_up(slot, tail)
+                ring_down(last_slot, ff_chunk)
+                ebuf[:, pl.ds(0, tail)] = hidden
+                for half in range(2):
+                    cp_wq[1][half].start()
+                cps[2].wait()
+                ring_down(slot, tail, send=True)
+            else:
+                for half in range(2):
+                    cp_wq[1][half].start()
+                ring_down(last_slot, ff_chunk, send=True)
+            cp_wo[1].start()
+        with scope("mwait"):
+            for n in range(ncol):
+                rc_m[n].wait()
+
+        def second_norm(rs):
+            acc = jnp.concatenate([macc[n, rs, :] + mrecv[n, rs, :] for n in range(ncol)], axis=1)
+            res = (hbuf[rs, :].astype(F32) + acc).astype(BF16)
+            hbuf[rs, :] = res
+            ubuf[rs, :] = normed(res.astype(F32))
+
+        with scope("norm2"):
+            row_loop(ctok, second_norm)
+        gout[0] = hbuf[my_rows, :]
+        cp_g.start()
+
+    pl.run_scoped(middle, pltpu.VMEM((width, ff_first), BF16), pltpu.VMEM((width, ff_first), BF16),
+                  pltpu.VMEM((ff_first, width), BF16))
     with scope("proj1"):
         project(1, ubuf)
     with scope("attn1"):
@@ -506,7 +543,7 @@
 def solution(mesh):
     axis_size = mesh.shape["cp"]
     nchip = axis_size // 2
-    ff_chunk, ff_slots = 512, 5
+    ff_first, ff_chunk, ff_slots = 384, 512, 5
     rows_spec = P(("dp", "cp"), None)
     cache_spec = P(("dp", "cp"), None, None)
     mat_spec = P(None, None)
@@ -531,8 +568,7 @@
             pltpu.VMEM((ctok, width), BF16),
             pltpu.VMEM((ctok, width), BF16),
             pltpu.VMEM((ctok, width), BF16),
-            pltpu.VMEM(w_k1.shape, BF16),
-            pltpu.VMEM(w_v1.shape, BF16),
+            pltpu.VMEM((width, 4 * hd), BF16),
             pltpu.VMEM((half_w, width), BF16),
             pltpu.VMEM((2, keys_tot, hd), BF16),
             pltpu.VMEM((2, hd, keys_tot), BF16),
@@ -540,15 +576,13 @@
             pltpu.VMEM((2 * cache_dev, hd), BF16),
             pltpu.VMEM((cache_dev, hd), BF16),
             pltpu.VMEM((hd, cache_dev), BF16),
-            pltpu.VMEM((2 * hd, hd), F32),
+            pltpu.VMEM((8 * hd, hd), F32),
             pltpu.VMEM((UNITS, rows, hd), BF16),
-            pltpu.VMEM((keys_tot, rows), F32),
-            pltpu.VMEM((keys_tot, rows), F32),
             pltpu.VMEM((8, rows), F32),
             pltpu.VMEM((8, rows), F32),
-            pltpu.VMEM((UNITS, hd + 8, rows), F32),
-            pltpu.VMEM((PAIRS, hd + 8, rows), F32),
-            pltpu.VMEM((2, PAIRS, hd + 8, rows), F32),
+            pltpu.VMEM((UNITS, 2 * hd + 8, ctok), F32),
+            pltpu.VMEM((PAIRS, 2 * hd + 8, ctok), F32),
+            pltpu.VMEM((2, PAIRS, 2 * hd + 8, ctok), F32),
             pltpu.VMEM((ctok, half_w), BF16),
             pltpu.VMEM((ncol, ctok, width // ncol), F32),
             pltpu.VMEM((ncol, ctok, width // ncol), F32),
@@ -556,14 +590,14 @@
             pltpu.VMEM((ff_slots, width, ff_chunk), BF16),
             pltpu.VMEM((ff_slots, width, ff_chunk), BF16),
             pltpu.VMEM((ff_slots, ff_chunk, width), BF16),
-            pltpu.VMEM((ctok, ff_chunk), BF16),
+            pltpu.VMEM((ctok, max(ff_first, ff_chunk)), BF16),
             pltpu.VMEM((ctok, hd), F32),
             pltpu.VMEM((ctok, hd), F32),
             pltpu.VMEM((2, width // hd, hd), BF16),
             pltpu.VMEM((2, kv_heads, hd), BF16),
             pltpu.VMEM((2, 2, 2 * tok, hd), BF16),
             pltpu.VMEM((2, tok, width), BF16),
-            pltpu.SemaphoreType.DMA((33,)),
+            pltpu.SemaphoreType.DMA((32,)),
             pltpu.SemaphoreType.DMA((3, ff_slots)),
             pltpu.SemaphoreType.DMA((65,)),
             pltpu.SemaphoreType.DMA((65,)),
@@ -571,7 +605,7 @@
         act = jax.ShapeDtypeStruct((tok, width), BF16)
         app = jax.ShapeDtypeStruct((kv_heads * tok, hd), BF16)
         outs = pl.pallas_call(
-            functools.partial(block_kernel, nchip, ff_chunk, ff_slots),
+            functools.partial(block_kernel, nchip, ff_first, ff_chunk, ff_slots),
             out_shape=(act, act, app, app, app, app),
             in_specs=[hbm] * 22,
             out_specs=(hbm,) * 6,

time: 99.2 us -> 92 us (0.927)
  Pallas kernels: 98.5 us -> 91.2 us
    pallas_call x1, Pallas kernels: 96.6 us -> 89.3 us  [forward(): pl.pallas_call(functools.partial(block_kernel, nchip, ff_first, ff_chunk,...]
where the time goes in v3:
time: 92 us; the launch traced here: 91.9 us
  Pallas kernels  91.2 us (99%)
    pallas_call x1, Pallas kernels, forward(): pl.pallas_call(functools.partial(block_kernel, nchip, ff_first, ff_chunk,...  89.3 us
    pallas_call x1, Pallas kernels, forward(): pl.pallas_call(copy_out, out_shape=[jax.ShapeDtypeStruct(arr.shape, arr.d...  1.9 us

profile of v3, /device:TPU:113, one launch (start us, length us, event | category | flops | bytes accessed | tf_op | source)
XLA Modules:
  0.0 91.9 jit_solution(3598427581642389379)
XLA Ops:
  0.6 89.3 %shard_map.253 = (bf16[64,2048]{1,0:T(8,128)(2,1)}, bf16[64,2048]{1,0:T(8,128)(2,1)}, bf16[128,128]{1,0:T(8,128)(2,1)}, bf16[128,128]{1,0:T(8,128)(2,1)}, bf16[1...) custom-call(bf16[64,2048]{1,0:T(8,128)(2,1)} %x_hbm.1, bf16[4096,128]{1,0:T(8,128)(2,1)} %bitcast.12, ...), custom_call_target="tpu_custom_call" | custom-call | tf_op jit(solution)/shard_map/pallas_call | solution.py:607
  90.0 1.9 %shard_map.254 = (bf16[64,2048]{1,0:T(8,128)(2,1)}, bf16[64,2048]{1,0:T(8,128)(2,1)}, bf16[128,128]{1,0:T(8,128)(2,1)}, bf16[128,128]{1,0:T(8,128)(2,1)}, bf16[1...) custom-call(bf16[64,2048]{1,0:T(8,128)(2,1)} %get-tuple-element.18.refs_0_, bf16[64,2048]{1,0:T(8,128)(2,1)} %get-tuple-element.19.refs_1_, ...), custom_call_target="tpu_custom_call" | custom-call | tf_op jit(solution)/shard_map/pallas_call | solution.py:617
